TPU v7x, 32 devices: a whole 2x2x4 slice. The times are simulated.
32 devices in a mesh: tensor: 4 (over x, core), dp: 8 (over z, y).
Axes of the slice: x: 2, y: 2, z: 4, core: 2. Of those that a mesh axis runs over, the one named last changes fastest.
Arguments:
- grads: bfloat16 [8, 4, 8192, 1024], P('dp', None, None, 'tensor'), may hold values from -6 to 6
- param: float32 [4, 8192, 1024], P(None, 'dp', 'tensor'), may hold values from -3 to 3
- q_m: bfloat16 [4, 8192, 1024], P(None, 'dp', 'tensor'), may hold values from -1 to 1
- m_scale: float32 [4], replicated, may hold values from 0.02 to 0.2
- q_v: bfloat16 [4, 8192, 1024], P(None, 'dp', 'tensor'), may hold values from 0.0009994507 to 1
- v_max: float32 [4, 8], P(None, 'tensor'), may hold values from 0.005 to 0.05
- v_exp: float32 [4, 8], P(None, 'tensor'), may hold values from 1 to 10
Outputs:
- new_param: float32 [4, 8192, 1024], P(None, 'dp', 'tensor')
- new_q_m: bfloat16 [4, 8192, 1024], P(None, 'dp', 'tensor')
- new_m_scale: float32 [4], replicated
- new_q_v: bfloat16 [4, 8192, 1024], P(None, 'dp', 'tensor')
- new_v_max: float32 [4, 8], P(None, 'tensor')
- new_v_exp: float32 [4, 8], P(None, 'tensor')
All inputs are finite; a program needn't handle non-finite values. Where the computation divides by a largest or mean magnitude, that divisor is 1e-20 or more.
Results may differ from a plain program's by a relative error of at most 0.001.
Values sent between devices are 32-bit elements; how exact they have to be, the bound alone decides.
A program may use at most 192 MiB of HBM per device.

v0:
```python
import functools

import jax
import jax.numpy as jnp
from jax import lax
from jax.experimental import pallas as pl
from jax.experimental.pallas import tpu as pltpu
from jax.sharding import PartitionSpec as P

MESH = pl.DeviceIdType.MESH
STEP = 32
Z_FIRST = 0.25


def kernel(n, peers, rows_a, rows_b, *refs):
    (grads, param, q_m, q_v, m_scale, v_max, v_exp,
     out_p, out_m, out_v, out_s,
     raw, a_cast, a_ring, a_side, b_cast, b_side, b_ring,
     par, qm, qv, m_new, v_new, stat, stat_in, peak, peak_in,
     raw_sem, in_sem, out_sem,
     a_send, a_recv, as_send, as_recv, bs_send, bs_recv, b_send, b_recv,
     st_send, st_recv, pk_send, pk_recv) = refs
    count, _, rows, width = grads.shape
    groups = v_max.shape[1]
    lanes = width // groups
    nz = n // 2
    me = lax.axis_index("dp")
    mt = lax.axis_index("tensor")
    y = lax.rem(me, 2)
    z = me // 2
    other = z * 2 + (1 - y)
    signs = (1, -1)
    a_off = (0, rows_a)
    b_off = (2 * rows_a, 2 * rows_a + rows_b)

    def at_z(offset):
        return lax.rem(z + (offset % nz), nz)

    def ring_to(s):
        return at_z(s) * 2 + y

    barrier = pltpu.get_barrier_semaphore()

    raws = [pltpu.make_async_copy(grads.at[t], raw.at[t % 3], raw_sem.at[t]) for t in range(count)]
    ins = [[pltpu.make_async_copy(src.at[t], dst.at[t], in_sem.at[t, i])
            for i, (src, dst) in enumerate(((q_m, qm), (q_v, qv), (param, par)))] for t in range(count)]
    for t in range(min(3, count)):
        raws[t].start()
    for t in range(count):
        for c in ins[t]:
            c.start()

    def greet(o, _):
        pl.semaphore_signal(barrier, inc=1, device_id={"dp": lax.rem(me + o, n)}, device_id_type=MESH)
        return 0
    lax.fori_loop(1, n, greet, 0)

    def greet_t(o, _):
        pl.semaphore_signal(barrier, inc=1, device_id={"tensor": lax.rem(mt + o, peers)}, device_id_type=MESH)
        return 0
    lax.fori_loop(1, peers, greet_t, 0)
    pl.semaphore_wait(barrier, n - 1 + peers - 1)

    unsent = {}

    def send(key, src, dst, s_sem, r_sem, to):
        c = pltpu.make_async_remote_copy(src_ref=src, dst_ref=dst, send_sem=s_sem, recv_sem=r_sem,
                                         device_id={"dp": to}, device_id_type=MESH)
        c.start()
        unsent[key] = c
        return c

    def sent(key):
        unsent.pop(key).wait_send()

    def loop(total, body):
        def one(i, _):
            body(pl.multiple_of(i * STEP, STEP))
            return 0
        lax.fori_loop(0, total // STEP, one, 0)

    def mine(t, k, side, at, i):
        return raw[t % 3, k * 2 + side, pl.ds(pl.multiple_of(at + i, STEP), STEP), :].astype(jnp.float32)

    live = {}

    def cast(t):
        raws[t].wait()
        for d, s in enumerate(signs):
            if t >= 2:
                sent(("a", t - 2, d, 0))
            k = at_z(-s)
            for side in range(2):
                def body(i):
                    a_cast[t % 2, d, side, pl.ds(i, STEP), :] = mine(t, k, side, a_off[d], i)
                loop(rows_a, body)
            live["a", t, d, 0] = send(("a", t, d, 0), a_cast.at[t % 2, d], a_ring.at[t, d, 0],
                                      a_send.at[t, d, 0], a_recv.at[t, d, 0], ring_to(s))
        for d, s in enumerate(signs):
            if t >= 2:
                sent(("bs", t - 2, d))

            def block(k, _):
                def body(i):
                    b_cast[t % 2, d, k, pl.ds(i, STEP), :] = mine(t, k, 1 - y, b_off[d], i)
                loop(rows_b, body)
                return 0
            lax.fori_loop(0, nz, block, 0)
            live["bs", t, d] = send(("bs", t, d), b_cast.at[t % 2, d], b_side.at[t, d],
                                    bs_send.at[t, d], bs_recv.at[t, d], other)

    def a_step(t, j):
        for d, s in enumerate(signs):
            live["a", t, d, j].wait_recv()
            k = at_z(-s * (j + 2))
            for side in range(2):
                def body(i):
                    at = (t, d, j, side, pl.ds(i, STEP), slice(None))
                    a_ring[at] = a_ring[at] + mine(t, k, side, a_off[d], i)
                loop(rows_a, body)
            if j < nz - 2:
                live["a", t, d, j + 1] = send(("a", t, d, j + 1), a_ring.at[t, d, j], a_ring.at[t, d, j + 1],
                                              a_send.at[t, d, j + 1], a_recv.at[t, d, j + 1], ring_to(s))
            else:
                live["as", t, d] = send(("as", t, d), a_ring.at[t, d, j, 1 - y], a_side.at[t, d],
                                        as_send.at[t, d], as_recv.at[t, d], other)

    def b_start(t):
        for d, s in enumerate(signs):
            live["bs", t, d].wait_recv()
            k = at_z(-s)

            def body(i):
                at = (t, d, k, pl.ds(i, STEP), slice(None))
                b_side[at] = b_side[at] + mine(t, k, y, b_off[d], i)
            loop(rows_b, body)
            live["b", t, d, 0] = send(("b", t, d, 0), b_side.at[t, d, k], b_ring.at[t, d, 0],
                                      b_send.at[t, d, 0], b_recv.at[t, d, 0], ring_to(s))

    def b_step(t, j):
        for d, s in enumerate(signs):
            live["b", t, d, j].wait_recv()
            if j == nz - 2:
                def total(i):
                    rows_i = pl.ds(i, STEP)
                    return b_ring[t, d, j, rows_i, :] + (b_side[t, d, z, rows_i, :] + mine(t, z, y, b_off[d], i))
                update(t, b_off[d], rows_b, total)
                continue
            k = at_z(-s * (j + 2))

            def body(i):
                at = (t, d, j, pl.ds(i, STEP), slice(None))
                b_ring[at] = b_ring[at] + (b_side[t, d, k, pl.ds(i, STEP), :] + mine(t, k, y, b_off[d], i))
            loop(rows_b, body)
            live["b", t, d, j + 1] = send(("b", t, d, j + 1), b_ring.at[t, d, j], b_ring.at[t, d, j + 1],
                                          b_send.at[t, d, j + 1], b_recv.at[t, d, j + 1], ring_to(s))

    def a_last(t):
        for c in ins[t]:
            c.wait()
        stat[t] = jnp.full(stat.shape[1:], -jnp.inf, jnp.float32)
        for d in range(2):
            live["as", t, d].wait_recv()

            def total(i):
                rows_i = pl.ds(i, STEP)
                return a_ring[t, d, nz - 2, y, rows_i, :] + a_side[t, d, rows_i, :]
            update(t, a_off[d], rows_a, total)

    def update(t, base, length, total):
        scale = m_scale[t]

        def fold(x):
            return jnp.max(x.reshape(STEP // 8, 8, lanes), axis=0)

        def one(it, carry):
            i = pl.multiple_of(it * STEP, STEP)
            whole = total(i) * (1.0 / n)
            rows_i = pl.ds(pl.multiple_of(base + i, STEP), STEP)
            top_m, tops, lows = carry
            new_tops, new_lows = [], []
            for g in range(groups):
                cols = slice(g * lanes, (g + 1) * lanes)
                grad = whole[:, cols]
                m_old = scale * qm[t, rows_i, cols].astype(jnp.float32)
                stored = qv[t, rows_i, cols].astype(jnp.float32)
                inv = 1.0 / jnp.full((1, lanes), v_exp[t, g], jnp.float32)
                v_old = v_max[t, g] * jnp.exp(jnp.log(stored) * inv)
                m = 0.9 * m_old + 0.1 * grad
                v = 0.95 * v_old + 0.05 * grad * grad
                w = par[t, rows_i, cols]
                par[t, rows_i, cols] = w - 0.02 * (m / (jnp.sqrt(v) + 1e-08) + 0.1 * w)
                m_new[t % 2, rows_i, cols] = m
                v_new[t % 2, rows_i, cols] = v
                top_m = jnp.maximum(top_m, fold(jnp.abs(m)))
                new_tops.append(jnp.maximum(tops[g], fold(v)))
                new_lows.append(jnp.maximum(lows[g], fold(-v)))
            return top_m, tuple(new_tops), tuple(new_lows)
        least = jnp.full((8, lanes), -jnp.inf, jnp.float32)
        top_m, tops, lows = lax.fori_loop(0, length // STEP, one, (least, (least,) * groups, (least,) * groups))
        for row, value in enumerate((top_m,) + tops + lows):
            stat[t, row:row + 1, :] = jnp.maximum(stat[t, row:row + 1, :], jnp.max(value, axis=0, keepdims=True))

    def stat_copy(t, o):
        return pltpu.make_async_remote_copy(
            src_ref=stat.at[t], dst_ref=stat_in.at[t, o], send_sem=st_send.at[t, o], recv_sem=st_recv.at[t, o],
            device_id={"dp": lax.rem(me + o, n)}, device_id_type=MESH)

    def peak_copy(t, o):
        return pltpu.make_async_remote_copy(
            src_ref=peak.at[t], dst_ref=peak_in.at[t, o], send_sem=pk_send.at[t, o], recv_sem=pk_recv.at[t, o],
            device_id={"tensor": lax.rem(mt + o, peers)}, device_id_type=MESH)

    def each(lo, hi, act):
        def one(o, _):
            act(o)
            return 0
        lax.fori_loop(lo, hi, one, 0)

    outs = []

    def give(src, dst, t, i):
        c = pltpu.make_async_copy(src.at[t], dst.at[t], out_sem.at[t, i])
        c.start()
        outs.append(c)

    def share(t):
        give(par, out_p, t, 0)
        each(1, n, lambda o: stat_copy(t, o).start())

    def finish(t):
        each(1, n, lambda o: stat_copy(t, o).wait_recv())
        best = lax.fori_loop(1, n, lambda o, b: jnp.maximum(b, stat_in[t, o]), stat[t])
        best = jnp.broadcast_to(jnp.max(best, axis=1, keepdims=True), best.shape)
        peak[t] = best
        each(1, peers, lambda o: peak_copy(t, o).start())
        exps, invs = [], []
        for g in range(groups):
            top = best[1 + g:2 + g, :]
            low = -best[1 + groups + g:2 + groups + g, :]
            exps.append(12.343 / jnp.maximum(jnp.log(top / low), 1.0))
            invs.append(1.0 / top)
            out_s[t, 1 + g:2 + g, :] = top
            out_s[t, 1 + groups + g:2 + groups + g, :] = exps[g]

        def body(i):
            for g in range(groups):
                at = (pl.ds(i, STEP), slice(g * lanes, (g + 1) * lanes))
                value = jnp.exp(exps[g] * jnp.log(v_new[(t % 2,) + at] * invs[g]))
                qv[(t,) + at] = value.astype(jnp.bfloat16)
        loop(rows, body)
        give(qv, out_v, t, 1)
        each(1, peers, lambda o: peak_copy(t, o).wait_recv())
        whole = lax.fori_loop(1, peers, lambda o, b: jnp.maximum(b, peak_in[t, o]), best)[0:1, :] + 1e-06
        out_s[t, 0:1, :] = whole
        inverse = 1.0 / whole

        def body_m(i):
            for g in range(groups):
                at = (pl.ds(i, STEP), slice(g * lanes, (g + 1) * lanes))
                qm[(t,) + at] = (m_new[(t % 2,) + at] * inverse).astype(jnp.bfloat16)
        loop(rows, body_m)
        give(qm, out_m, t, 2)

    cast(0)
    for p in range(count + 1):
        if p + 1 < count:
            cast(p + 1)
        if p >= 1:
            b_start(p - 1)
        for j in range(nz - 1):
            if p < count:
                a_step(p, j)
            if p >= 1 and j == nz - 2:
                a_last(p - 1)
            if p >= 1:
                b_step(p - 1, j)
        if p >= 1:
            if p + 2 < count:
                raws[p + 2].start()
            share(p - 1)
        if p >= 2:
            finish(p - 2)
    finish(count - 1)

    for key in list(unsent):
        sent(key)
    for t in range(count):
        each(1, n, lambda o: stat_copy(t, o).wait_send())
        each(1, peers, lambda o: peak_copy(t, o).wait_send())
    for c in outs:
        c.wait()


def on_device(n, peers, grads, param, q_m, m_scale, q_v, v_max, v_exp):
    count, rows, width = q_m.shape
    groups = v_max.shape[1]
    lanes = width // groups
    nz = n // 2
    rows_a = min(max(STEP, round(rows * Z_FIRST / 2 / STEP) * STEP), rows // 2 - STEP)
    rows_b = rows // 2 - rows_a
    kinds = -(-(1 + 2 * groups) // 8) * 8
    f32, bf16 = jnp.float32, jnp.bfloat16
    dma = pltpu.SemaphoreType.DMA
    hbm = pl.BlockSpec(memory_space=pl.ANY)
    smem = pl.BlockSpec(memory_space=pltpu.SMEM)
    new_param, new_q_m, new_q_v, stats = pl.pallas_call(
        functools.partial(kernel, n, peers, rows_a, rows_b),
        out_shape=(
            jax.ShapeDtypeStruct(param.shape, f32),
            jax.ShapeDtypeStruct(q_m.shape, bf16),
            jax.ShapeDtypeStruct(q_v.shape, bf16),
            jax.ShapeDtypeStruct((count, kinds, lanes), f32),
        ),
        in_specs=[hbm] * 4 + [smem] * 3,
        out_specs=(hbm, hbm, hbm, pl.BlockSpec(memory_space=pltpu.VMEM)),
        scratch_shapes=[
            pltpu.VMEM((3, n, rows, width), bf16),
            pltpu.VMEM((2, 2, 2, rows_a, width), f32),
            pltpu.VMEM((count, 2, nz - 1, 2, rows_a, width), f32),
            pltpu.VMEM((count, 2, rows_a, width), f32),
            pltpu.VMEM((2, 2, nz, rows_b, width), f32),
            pltpu.VMEM((count, 2, nz, rows_b, width), f32),
            pltpu.VMEM((count, 2, nz - 1, rows_b, width), f32),
            pltpu.VMEM(param.shape, f32),
            pltpu.VMEM(q_m.shape, bf16),
            pltpu.VMEM(q_v.shape, bf16),
            pltpu.VMEM((2, rows, width), f32),
            pltpu.VMEM((2, rows, width), f32),
            pltpu.VMEM((count, kinds, lanes), f32),
            pltpu.VMEM((count, n, kinds, lanes), f32),
            pltpu.VMEM((count, kinds, lanes), f32),
            pltpu.VMEM((count, peers, kinds, lanes), f32),
            dma((count,)), dma((count, 3)), dma((count, 3)),
            dma((count, 2, nz - 1)), dma((count, 2, nz - 1)),
            dma((count, 2)), dma((count, 2)),
            dma((count, 2)), dma((count, 2)),
            dma((count, 2, nz - 1)), dma((count, 2, nz - 1)),
            dma((count, n)), dma((count, n)),
            dma((count, peers)), dma((count, peers)),
        ],
        compiler_params=pltpu.CompilerParams(
            collective_id=0, has_side_effects=True, vmem_limit_bytes=67043328
        ),
    )(grads[0].reshape(count, n, rows, width), param, q_m, q_v, m_scale, v_max, v_exp)
    new_m_scale = stats[:, 0, 0]
    group_top = stats[:, 1:1 + groups, 0]
    new_v_exp = stats[:, 1 + groups:1 + 2 * groups, 0]
    return new_param, new_q_m, new_m_scale, new_q_v, group_top, new_v_exp


def solution(mesh):
    in_specs = (
        P("dp", None, None, "tensor"),
        P(None, "dp", "tensor"),
        P(None, "dp", "tensor"),
        P(),
        P(None, "dp", "tensor"),
        P(None, "tensor"),
        P(None, "tensor"),
    )
    out_specs = (
        P(None, "dp", "tensor"),
        P(None, "dp", "tensor"),
        P(),
        P(None, "dp", "tensor"),
        P(None, "tensor"),
        P(None, "tensor"),
    )
    return jax.shard_map(
        functools.partial(on_device, mesh.shape["dp"], mesh.shape["tensor"]),
        mesh=mesh, in_specs=in_specs, out_specs=out_specs, check_vma=False
    )
```

profile of v0, /device:TPU:0, one launch (start us, length us, event | category | flops | bytes accessed | tf_op | source)
XLA Modules:
  0.0 404.2 jit_solution(12273424647282277555)
XLA Ops:
  0.6 1.3 copy.17.refs_5_
  2.0 1.3 copy.18.refs_6_
  3.3 389.1 %shard_map.118 = (f32[4,1024,256]{2,1,0:T(8,128)}, bf16[4,1024,256]{2,1,0:T(8,128)(2,1)}, bf16[4,1024,256]{2,1,0:T(8,128)(2,1)}, f32[4,8,128]{2,1,0:T(8,128)}) custom-call(bf16[4,8,1024,256]{3,2,1,0:T(8,128)(2,1)} %bitcast.3, f32[4,1024,256]{2,1,0:T(8,128)} %refs_1_.1, bf16[4,1024,256]{2,1,0:T(8,128)(2,1)} %refs_2_.1, bf16[4,1024,256]{2,1,0:T(8,128)(2,1)} %refs_3_.1, ...), custom_call_target="tpu_custom_call" | custom-call | tf_op jit(solution)/shard_map/pallas_call | solution.py:307
  392.4 0.8 fusion
  393.2 0.7 copy.19
  393.8 0.7 copy.20
  394.5 1.3 slice_reduce_fusion
  395.8 0.0 copy-start.1
  395.8 4.7 %copy.24 = f32[4,1024,256]{2,1,0:T(8,128)} copy(f32[4,1024,256]{2,1,0:T(8,128)} %get-tuple-element.22) | data formatting | bytes 8388608
  400.6 0.0 copy-done.1
  400.6 0.0 copy-start
  400.6 1.3 copy.25
  401.9 1.0 copy-done
  402.9 1.3 copy.26
Async XLA Ops:
  395.8 4.7 %copy-start.1 = (bf16[4,1024,256]{2,1,0:T(8,128)(2,1)S(1)}, bf16[4,1024,256]{2,1,0:T(8,128)(2,1)}, u32[]{:S(2)}) copy-start(bf16[4,1024,256]{2,1,0:T(8,128)(2,1)} %get-tuple-element.23) | copy-start | bytes 6291460
  400.6 2.3 copy-start
where the time goes:
time: 405 us; the launch traced here: 404 us
  Pallas kernels  389 us (96%)
  local copies, waits for them, and re-layouts  14.5 us (4%)
    pallas_call x1, Pallas kernels, on_device(): pl.pallas_call(functools.partial(kernel, n, peers, rows_a, rows_b), out_s...  389 us
    unnamed x9, local copies, waits for them, and re-layouts  11.1 us

commit v1 on v0

v1 whole, which is shorter than its diff:
```python
import functools

import jax
import jax.numpy as jnp
from jax import lax
from jax.experimental import pallas as pl
from jax.experimental.pallas import tpu as pltpu
from jax.sharding import PartitionSpec as P

MESH = pl.DeviceIdType.MESH
STEP = 32
SPLIT = 1
SLOTS = 3
RING = 4
LEAD = 5
LAG_A = 4
LAG_B = 5
LAG_B_INNER = 9
LAG_UPDATE = 5
LAG_FINISH = 3
LAG_SCALE = 2


def kernel(n, peers, *refs):
    (grads, param, q_m, q_v, m_scale, v_max, v_exp,
     out_p, out_m, out_v, out_s,
     raw, y_cast, a_cast, y_in, z_in, s_out, s_in,
     par, qm, qv, m_new, v_new, stat, stat_in, peak, peak_in,
     raw_sem, in_sem, out_sem, y_send, y_recv, z_send, z_recv, s_send, s_recv,
     st_send, st_recv, pk_send, pk_recv) = refs
    count, _, rows, width = grads.shape
    groups = v_max.shape[1]
    lanes = width // groups
    nz = n // 2
    chunk = rows // (8 * SPLIT)
    step = min(STEP, chunk)
    wide = 7 * SPLIT
    tall = 4 * SPLIT
    sides = 2 * SPLIT
    period = wide * nz + sides
    me = lax.axis_index("dp")
    mt = lax.axis_index("tensor")
    y = lax.rem(me, 2)
    z = me // 2
    half = z // (nz // 2)
    zm = z + half * (nz - 1 - 2 * z)
    is_outer = zm == 0
    is_inner = zm == 1
    inner = 1 + half * (nz - 3)

    def is_end(d):
        return 1 - (lax.rem(d, nz - 1) + nz - 2) // (nz - 1)

    def n_b(d):
        return SPLIT * (7 - is_end(d))

    def n_a(d):
        return SPLIT * (1 + is_end(d))

    def order(i):
        low = jnp.minimum(zm, 1)
        d = nz - 1 + low - i
        d = d - low * jnp.where(d <= zm, 1, 0)
        d = jnp.where((i == 0) & (zm > 0), 0, d)
        d = jnp.where(i == nz - 1, zm, d)
        return d + half * (nz - 1 - 2 * d)

    def through(d):
        return nz - 2 + d - 2 * (1 - half)

    barrier = pltpu.get_barrier_semaphore()

    def raw_copy(t):
        return pltpu.make_async_copy(grads.at[t], raw.at[t], raw_sem.at[t])

    def in_copies(t):
        return [pltpu.make_async_copy(src.at[t], dst.at[t], in_sem.at[t, i])
                for i, (src, dst) in enumerate(((q_m, qm), (q_v, qv), (param, par)))]

    def out_copy(src, dst, t, i):
        return pltpu.make_async_copy(src.at[t], dst.at[t], out_sem.at[t, i])

    for t in range(count):
        raw_copy(t).start()
    for t in range(count):
        for c in in_copies(t):
            c.start()

    def greet(o, _):
        pl.semaphore_signal(barrier, inc=1, device_id={"dp": lax.rem(me + o, n)}, device_id_type=MESH)
        return 0
    lax.fori_loop(1, n, greet, 0)

    def greet_t(o, _):
        pl.semaphore_signal(barrier, inc=1, device_id={"tensor": lax.rem(mt + o, peers)}, device_id_type=MESH)
        return 0
    lax.fori_loop(1, peers, greet_t, 0)
    pl.semaphore_wait(barrier, n - 1 + peers - 1)

    def remote(src, dst, s_sem, r_sem, to):
        return pltpu.make_async_remote_copy(src_ref=src, dst_ref=dst, send_sem=s_sem, recv_sem=r_sem,
                                            device_id={"dp": to}, device_id_type=MESH)

    def loop(body):
        def one(i, _):
            body(pl.ds(pl.multiple_of(i * step, step), step))
            return 0
        lax.fori_loop(0, chunk // step, one, 0)

    def mine(t, d, side, c, at):
        first = pl.multiple_of(c * chunk + at.start, step)
        return raw[t, d * 2 + side, pl.ds(first, step), :].astype(jnp.float32)

    def y_copy(t, d, c, ring):
        s = lax.rem(t, SLOTS)
        return remote(y_cast.at[ring], y_in.at[s, d, c], y_send.at[ring], y_recv.at[s, d, c], z * 2 + 1 - y)

    def s_copy(t, c):
        s = lax.rem(t, SLOTS)
        h = lax.rem(t, 2)
        return remote(s_out.at[h, c], s_in.at[s, c], s_send.at[h, c], s_recv.at[s, c], z * 2 + 1 - y)

    def z_wait(t, where, c):
        s = lax.rem(t, SLOTS)
        remote(z_in.at[s, where, c], z_in.at[s, where, c], z_send.at[0, 0], z_recv.at[s, where, c], me).wait_recv()

    def landed(t, c):
        for k in range(nz - 2):
            if nz > 4:
                @pl.when((zm <= 1) | (z != k + 1))
                def _():
                    z_wait(t, k, c)
            else:
                z_wait(t, k, c)

    def gathered(t, c, at):
        s = lax.rem(t, SLOTS)
        total = None
        for k in range(nz - 2):
            part = z_in[s, k, c, at, :]
            if nz > 4:
                part = jnp.where((zm <= 1) | (z != k + 1), part, 0.0)
            total = part if total is None else total + part
        return total

    def z_go(t, src, d, c, sem):
        s = lax.rem(t, SLOTS)
        to = jnp.where(is_outer, inner, d)
        where = jnp.where(is_outer, jnp.where(d == inner, d - 1, through(d)), z - 1)
        remote(src, z_in.at[s, where, c], sem, z_recv.at[s, where, c], to * 2 + y).start()

    def z_sent(sem):
        remote(a_cast.at[0, 0], a_cast.at[0, 0], sem, z_recv.at[0, 0, 0], me).wait_send()

    def y_job(t, i, c, ring, full):
        d = order(i)

        @pl.when(full)
        def _():
            y_copy(t, d, c, ring).wait_send()

        def body(at):
            y_cast[ring, at, :] = mine(t, d, 1 - y, c, at)
        loop(body)
        y_copy(t, d, c, ring).start()

    def s_job(t, c):
        h = lax.rem(t, 2)

        @pl.when(t >= 2)
        def _():
            s_copy(t, c).wait_send()
        j = n_b(z) + (1 - y) * n_a(z) + c
        landed(t, j)

        def body(at):
            s_out[h, c, at, :] = gathered(t, j, at) + mine(t, z, 1 - y, n_b(z) + c, at)
        loop(body)
        s_copy(t, c).start()

    def a_job(t, i, j):
        s = lax.rem(t, SLOTS)
        d = order(i)
        side = j // n_a(d)
        c = n_b(d) + lax.rem(j, n_a(d))
        k = n_b(d) + j
        sem = z_send.at[i, wide + j]

        @pl.when(t > 0)
        def _():
            z_sent(sem)
        relay = is_inner & (i > 0)

        @pl.when(relay)
        def _():
            w = through(d)
            z_wait(t, w, k)

            def body(at):
                z_in[s, w, k, at, :] = z_in[s, w, k, at, :] + mine(t, d, side, c, at)
            loop(body)
            z_go(t, z_in.at[s, w, k], d, k, sem)

        @pl.when(jnp.logical_not(relay))
        def _():
            def body(at):
                a_cast[i, j, at, :] = mine(t, d, side, c, at)
            loop(body)
            z_go(t, a_cast.at[i, j], d, k, sem)

    def b_job(t, i, c):
        s = lax.rem(t, SLOTS)
        d = order(i)
        sem = z_send.at[i, c]

        @pl.when(t > 0)
        def _():
            z_sent(sem)
        y_copy(t, d, c, 0).wait_recv()
        relay = is_inner & (i > 0)

        @pl.when(relay)
        def _():
            w = through(d)
            z_wait(t, w, c)

            def body(at):
                z_in[s, w, c, at, :] = z_in[s, w, c, at, :] + (y_in[s, d, c, at, :] + mine(t, d, y, c, at))
            loop(body)
            z_go(t, z_in.at[s, w, c], d, c, sem)

        @pl.when(jnp.logical_not(relay))
        def _():
            def body(at):
                y_in[s, d, c, at, :] = y_in[s, d, c, at, :] + mine(t, d, y, c, at)
            loop(body)
            z_go(t, y_in.at[s, d, c], d, c, sem)

    def update(t, c, total):
        scale = m_scale[t]
        h = lax.rem(t, 2)

        def fold(x):
            return jnp.max(x.reshape(step // 8, 8, lanes), axis=0)

        def one(it, carry):
            at = pl.ds(pl.multiple_of(it * step, step), step)
            whole = total(at) * (1.0 / n)
            rows_i = pl.ds(pl.multiple_of(c * chunk + it * step, step), step)
            top_m, tops, lows = carry
            new_tops, new_lows = [], []
            for g in range(groups):
                cols = slice(g * lanes, (g + 1) * lanes)
                grad = whole[:, cols]
                m_old = scale * qm[t, rows_i, cols].astype(jnp.float32)
                stored = qv[t, rows_i, cols].astype(jnp.float32)
                inv = 1.0 / jnp.full((1, lanes), v_exp[t, g], jnp.float32)
                v_old = v_max[t, g] * jnp.exp(jnp.log(stored) * inv)
                m = 0.9 * m_old + 0.1 * grad
                v = 0.95 * v_old + 0.05 * grad * grad
                w = par[t, rows_i, cols]
                par[t, rows_i, cols] = w - 0.02 * (m / (jnp.sqrt(v) + 1e-08) + 0.1 * w)
                m_new[h, rows_i, cols] = m
                v_new[h, rows_i, cols] = v
                top_m = jnp.maximum(top_m, fold(jnp.abs(m)))
                new_tops.append(jnp.maximum(tops[g], fold(v)))
                new_lows.append(jnp.maximum(lows[g], fold(-v)))
            return top_m, tuple(new_tops), tuple(new_lows)
        least = jnp.full((8, lanes), -jnp.inf, jnp.float32)
        top_m, tops, lows = lax.fori_loop(0, chunk // step, one, (least, (least,) * groups, (least,) * groups))
        for row, value in enumerate((top_m,) + tops + lows):
            stat[t, row:row + 1, :] = jnp.maximum(stat[t, row:row + 1, :], jnp.max(value, axis=0, keepdims=True))

    def update_a(t, c):
        s = lax.rem(t, SLOTS)

        @pl.when(c == 0)
        def _():
            for copy in in_copies(t):
                copy.wait()
            stat[t] = jnp.full(stat.shape[1:], -jnp.inf, jnp.float32)
        j = n_b(z) + y * n_a(z) + c
        landed(t, j)
        s_copy(t, c).wait_recv()
        update(t, n_b(z) + c,
               lambda at: gathered(t, j, at) + mine(t, z, y, n_b(z) + c, at) + s_in[s, c, at, :])

    def update_b(t, c):
        s = lax.rem(t, SLOTS)
        y_copy(t, z, c, 0).wait_recv()
        landed(t, c)
        update(t, c, lambda at: gathered(t, c, at) + (y_in[s, z, c, at, :] + mine(t, z, y, c, at)))

    def stat_copy(t, o):
        return pltpu.make_async_remote_copy(
            src_ref=stat.at[t], dst_ref=stat_in.at[t, o], send_sem=st_send.at[t, o], recv_sem=st_recv.at[t, o],
            device_id={"dp": lax.rem(me + o, n)}, device_id_type=MESH)

    def peak_copy(t, o):
        return pltpu.make_async_remote_copy(
            src_ref=peak.at[t], dst_ref=peak_in.at[t, o], send_sem=pk_send.at[t, o], recv_sem=pk_recv.at[t, o],
            device_id={"tensor": lax.rem(mt + o, peers)}, device_id_type=MESH)

    def each(lo, hi, act):
        def one(o, _):
            act(o)
            return 0
        lax.fori_loop(lo, hi, one, 0)

    def share(t):
        out_copy(par, out_p, t, 0).start()
        each(1, n, lambda o: stat_copy(t, o).start())

    def all_rows(body):
        def one(i, _):
            body(pl.ds(pl.multiple_of(i * STEP, STEP), STEP))
            return 0
        lax.fori_loop(0, rows // STEP, one, 0)

    def finish(t):
        h = lax.rem(t, 2)
        each(1, n, lambda o: stat_copy(t, o).wait_recv())
        best = lax.fori_loop(1, n, lambda o, b: jnp.maximum(b, stat_in[t, o]), stat[t])
        best = jnp.broadcast_to(jnp.max(best, axis=1, keepdims=True), best.shape)
        peak[t] = best
        each(1, peers, lambda o: peak_copy(t, o).start())
        exps, invs = [], []
        for g in range(groups):
            top = best[1 + g:2 + g, :]
            low = -best[1 + groups + g:2 + groups + g, :]
            exps.append(12.343 / jnp.maximum(jnp.log(top / low), 1.0))
            invs.append(1.0 / top)
            out_s[t, 1 + g:2 + g, :] = top
            out_s[t, 1 + groups + g:2 + groups + g, :] = exps[g]

        def body(at):
            for g in range(groups):
                cols = slice(g * lanes, (g + 1) * lanes)
                value = jnp.exp(exps[g] * jnp.log(v_new[h, at, cols] * invs[g]))
                qv[t, at, cols] = value.astype(jnp.bfloat16)
        all_rows(body)
        out_copy(qv, out_v, t, 1).start()

    def scale(t):
        h = lax.rem(t, 2)
        each(1, peers, lambda o: peak_copy(t, o).wait_recv())
        whole = lax.fori_loop(1, peers, lambda o, b: jnp.maximum(b, peak_in[t, o]), peak[t])[0:1, :] + 1e-06
        out_s[t, 0:1, :] = whole
        inverse = 1.0 / whole

        def body(at):
            for g in range(groups):
                cols = slice(g * lanes, (g + 1) * lanes)
                qm[t, at, cols] = (m_new[h, at, cols] * inverse).astype(jnp.bfloat16)
        all_rows(body)
        out_copy(qm, out_m, t, 2).start()

    lag_a = jnp.where(is_inner, LAG_A, -LEAD)
    lag_b = jnp.where(is_inner, LAG_B_INNER, LAG_B)
    own = wide * (nz - 1) + sides

    def place(g, lag):
        g = g - lag
        ok = (g >= 0) & (g < count * period)
        g = jnp.clip(g, 0, count * period - 1)
        return ok, g // period, lax.rem(g, period)

    def one(it, sent):
        g = it - LEAD
        ok, t, p = place(g, -LEAD)

        @pl.when(ok & (p == 0))
        def _():
            raw_copy(t).wait()

        ok, t, p = place(g, lag_a)
        i, j = jnp.minimum(p // tall, nz - 2), lax.rem(p, tall)

        @pl.when(ok & (p < tall * (nz - 1)) & (j < 2 * n_a(order(i))))
        def _():
            a_job(t, i, j)

        ok, t, p = place(g, 0)
        tail = p >= own
        i = jnp.where(tail, nz - 1, p // wide)
        c = jnp.where(tail, p - own, lax.rem(p, wide))
        live = ok & (tail | (p < own - sides)) & (c < n_b(order(i)))

        @pl.when(live)
        def _():
            y_job(t, i, c, lax.rem(sent, RING), sent >= RING)
        sent = sent + jnp.where(live, 1, 0)
        c = p - (own - sides)

        @pl.when(ok & (c >= 0) & (c < n_a(z)) & (p < own))
        def _():
            s_job(t, c)

        ok, t, p = place(g, lag_b)
        i, c = p // wide, lax.rem(p, wide)

        @pl.when(ok & (p < own - sides) & (c < n_b(order(i))))
        def _():
            b_job(t, i, c)

        ok, t, p = place(g, LAG_UPDATE)
        c = p - (own - sides)

        @pl.when(ok & (c >= 0) & (c < n_a(z)) & (p < own))
        def _():
            update_a(t, c)
        c = p - own

        @pl.when(ok & (c >= 0) & (c < n_b(z)))
        def _():
            update_b(t, c)

        @pl.when(ok & (p == period - 1))
        def _():
            share(t)

        ok, t, p = place(g, LAG_UPDATE + LAG_FINISH)

        @pl.when(ok & (p == period - 1))
        def _():
            finish(t)

        ok, t, p = place(g, LAG_UPDATE + LAG_FINISH + LAG_SCALE)

        @pl.when(ok & (p == period - 1))
        def _():
            scale(t)
        return sent

    steps = LEAD + count * period + LAG_UPDATE + LAG_FINISH + LAG_SCALE
    lax.fori_loop(0, steps, one, 0)

    each(0, RING, lambda r: y_copy(0, 0, 0, r).wait_send())

    def drain(i, _):
        d = order(i)
        each(0, n_b(d), lambda c: z_sent(z_send.at[i, c]))
        each(0, 2 * n_a(d), lambda j: z_sent(z_send.at[i, wide + j]))
        return 0
    lax.fori_loop(0, nz - 1, drain, 0)
    for t in range(max(0, count - 2), count):
        each(0, n_a(z), lambda c: s_copy(t, c).wait_send())
    for t in range(count):
        each(1, n, lambda o: stat_copy(t, o).wait_send())
        each(1, peers, lambda o: peak_copy(t, o).wait_send())
        out_copy(par, out_p, t, 0).wait()
        out_copy(qv, out_v, t, 1).wait()
        out_copy(qm, out_m, t, 2).wait()


def on_device(n, peers, grads, param, q_m, m_scale, q_v, v_max, v_exp):
    count, rows, width = q_m.shape
    groups = v_max.shape[1]
    lanes = width // groups
    nz = n // 2
    chunk = rows // (8 * SPLIT)
    wide, tall, deep = 7 * SPLIT, 4 * SPLIT, 10 * SPLIT
    kinds = -(-(1 + 2 * groups) // 8) * 8
    f32, bf16 = jnp.float32, jnp.bfloat16
    dma = pltpu.SemaphoreType.DMA
    hbm = pl.BlockSpec(memory_space=pl.ANY)
    smem = pl.BlockSpec(memory_space=pltpu.SMEM)
    new_param, new_q_m, new_q_v, stats = pl.pallas_call(
        functools.partial(kernel, n, peers),
        out_shape=(
            jax.ShapeDtypeStruct(param.shape, f32),
            jax.ShapeDtypeStruct(q_m.shape, bf16),
            jax.ShapeDtypeStruct(q_v.shape, bf16),
            jax.ShapeDtypeStruct((count, kinds, lanes), f32),
        ),
        in_specs=[hbm] * 4 + [smem] * 3,
        out_specs=(hbm, hbm, hbm, pl.BlockSpec(memory_space=pltpu.VMEM)),
        scratch_shapes=[
            pltpu.VMEM((count, n, rows, width), bf16),
            pltpu.VMEM((RING, chunk, width), f32),
            pltpu.VMEM((nz - 1, tall, chunk, width), f32),
            pltpu.VMEM((SLOTS, nz, wide, chunk, width), f32),
            pltpu.VMEM((SLOTS, 2 * (nz - 2), deep, chunk, width), f32),
            pltpu.VMEM((2, 2 * SPLIT, chunk, width), f32),
            pltpu.VMEM((SLOTS, 2 * SPLIT, chunk, width), f32),
            pltpu.VMEM(param.shape, f32),
            pltpu.VMEM(q_m.shape, bf16),
            pltpu.VMEM(q_v.shape, bf16),
            pltpu.VMEM((2, rows, width), f32),
            pltpu.VMEM((2, rows, width), f32),
            pltpu.VMEM((count, kinds, lanes), f32),
            pltpu.VMEM((count, n, kinds, lanes), f32),
            pltpu.VMEM((count, kinds, lanes), f32),
            pltpu.VMEM((count, peers, kinds, lanes), f32),
            dma((count,)), dma((count, 3)), dma((count, 3)),
            dma((RING,)), dma((SLOTS, nz, wide)),
            dma((nz - 1, wide + tall)), dma((SLOTS, 2 * (nz - 2), deep)),
            dma((2, 2 * SPLIT)), dma((SLOTS, 2 * SPLIT)),
            dma((count, n)), dma((count, n)),
            dma((count, peers)), dma((count, peers)),
        ],
        compiler_params=pltpu.CompilerParams(
            collective_id=0, has_side_effects=True, vmem_limit_bytes=67043328
        ),
    )(grads[0].reshape(count, n, rows, width), param, q_m, q_v, m_scale, v_max, v_exp)
    new_m_scale = stats[:, 0, 0]
    group_top = stats[:, 1:1 + groups, 0]
    new_v_exp = stats[:, 1 + groups:1 + 2 * groups, 0]
    return new_param, new_q_m, new_m_scale, new_q_v, group_top, new_v_exp


def solution(mesh):
    in_specs = (
        P("dp", None, None, "tensor"),
        P(None, "dp", "tensor"),
        P(None, "dp", "tensor"),
        P(),
        P(None, "dp", "tensor"),
        P(None, "tensor"),
        P(None, "tensor"),
    )
    out_specs = (
        P(None, "dp", "tensor"),
        P(None, "dp", "tensor"),
        P(),
        P(None, "dp", "tensor"),
        P(None, "tensor"),
        P(None, "tensor"),
    )
    return jax.shard_map(
        functools.partial(on_device, mesh.shape["dp"], mesh.shape["tensor"]),
        mesh=mesh, in_specs=in_specs, out_specs=out_specs, check_vma=False
    )
```

time: 405 us -> 359 us (0.89)
  Pallas kernels: 389 us -> 343 us
    pallas_call x1, Pallas kernels: 389 us -> 343 us  [on_device(): pl.pallas_call(functools.partial(kernel, n, peers), out_shape=(jax.ShapeD...]
where the time goes in v1:
time: 359 us; the launch traced here: 358 us
  Pallas kernels  343 us (96%)
  local copies, waits for them, and re-layouts  14.5 us (4%)
    pallas_call x1, Pallas kernels, on_device(): pl.pallas_call(functools.partial(kernel, n, peers), out_shape=(jax.ShapeD...  343 us
    unnamed x9, local copies, waits for them, and re-layouts  11.1 us

profile of v1, /device:TPU:0, one launch (start us, length us, event | category | flops | bytes accessed | tf_op | source)
XLA Modules:
  0.0 358.4 jit_solution(7203577168009127799)
XLA Ops:
  0.6 1.3 copy.17.refs_5_
  2.0 1.3 copy.18.refs_6_
  3.3 343.3 %shard_map.118 = (f32[4,1024,256]{2,1,0:T(8,128)}, bf16[4,1024,256]{2,1,0:T(8,128)(2,1)}, bf16[4,1024,256]{2,1,0:T(8,128)(2,1)}, f32[4,8,128]{2,1,0:T(8,128)}) custom-call(bf16[4,8,1024,256]{3,2,1,0:T(8,128)(2,1)} %bitcast.3, f32[4,1024,256]{2,1,0:T(8,128)} %refs_1_.1, bf16[4,1024,256]{2,1,0:T(8,128)(2,1)} %refs_2_.1, bf16[4,1024,256]{2,1,0:T(8,128)(2,1)} %refs_3_.1, ...), custom_call_target="tpu_custom_call" | custom-call | tf_op jit(solution)/shard_map/pallas_call | solution.py:468
  346.6 0.8 fusion
  347.4 0.7 copy.19
  348.0 0.7 copy.20
  348.7 1.3 slice_reduce_fusion
  350.0 0.0 copy-start.1
  350.0 4.7 %copy.24 = f32[4,1024,256]{2,1,0:T(8,128)} copy(f32[4,1024,256]{2,1,0:T(8,128)} %get-tuple-element.22) | data formatting | bytes 8388608
  354.7 0.0 copy-done.1
  354.7 0.0 copy-start
  354.7 1.3 copy.25
  356.1 1.0 copy-done
  357.1 1.3 copy.26
Async XLA Ops:
  350.0 4.7 %copy-start.1 = (bf16[4,1024,256]{2,1,0:T(8,128)(2,1)S(1)}, bf16[4,1024,256]{2,1,0:T(8,128)(2,1)}, u32[]{:S(2)}) copy-start(bf16[4,1024,256]{2,1,0:T(8,128)(2,1)} %get-tuple-element.23) | copy-start | bytes 6291460
  354.7 2.3 copy-start

commit v2 on v1

--- a/solution.py
+++ b/solution.py
@@ -1,4 +1,5 @@
 import functools
+import math
 
 import jax
 import jax.numpy as jnp
@@ -9,27 +10,30 @@
 
 MESH = pl.DeviceIdType.MESH
 STEP = 32
+LONG = 128
 SPLIT = 1
 SLOTS = 3
 RING = 4
-LEAD = 5
+Z_RING = 16
+LEAD = 1
 LAG_A = 4
 LAG_B = 5
 LAG_B_INNER = 9
 LAG_UPDATE = 5
-LAG_FINISH = 3
-LAG_SCALE = 2
+LAG_FINISH = 10
+LAG_SCALE = 5
+SPARE = 1 << 20
 
 
 def kernel(n, peers, *refs):
     (grads, param, q_m, q_v, m_scale, v_max, v_exp,
-     out_p, out_m, out_v, out_s,
+     par, qm, qv, m_new, v_new, out_s,
      raw, y_cast, a_cast, y_in, z_in, s_out, s_in,
-     par, qm, qv, m_new, v_new, stat, stat_in, peak, peak_in,
-     raw_sem, in_sem, out_sem, y_send, y_recv, z_send, z_recv, s_send, s_recv,
+     stat, stat_in, peak, peak_in,
+     raw_sem, in_sem, y_send, y_recv, z_send, z_recv, s_send, s_recv,
      st_send, st_recv, pk_send, pk_recv) = refs
     count, _, rows, width = grads.shape
-    groups = v_max.shape[1]
+    groups = v_max.shape[0]
     lanes = width // groups
     nz = n // 2
     chunk = rows // (8 * SPLIT)
@@ -70,21 +74,12 @@
 
     barrier = pltpu.get_barrier_semaphore()
 
-    def raw_copy(t):
-        return pltpu.make_async_copy(grads.at[t], raw.at[t], raw_sem.at[t])
-
-    def in_copies(t):
-        return [pltpu.make_async_copy(src.at[t], dst.at[t], in_sem.at[t, i])
-                for i, (src, dst) in enumerate(((q_m, qm), (q_v, qv), (param, par)))]
-
-    def out_copy(src, dst, t, i):
-        return pltpu.make_async_copy(src.at[t], dst.at[t], out_sem.at[t, i])
-
-    for t in range(count):
-        raw_copy(t).start()
-    for t in range(count):
-        for c in in_copies(t):
-            c.start()
+    raws = [pltpu.make_async_copy(grads.at[at], raw.at[at], raw_sem.at[i])
+            for i, at in enumerate((pl.ds(0, 1), pl.ds(1, count - 1)))]
+    ins = [pltpu.make_async_copy(src, dst, in_sem.at[i])
+           for i, (src, dst) in enumerate(((q_m, qm), (q_v, qv), (param, par)))]
+    for c in raws + ins:
+        c.start()
 
     def greet(o, _):
         pl.semaphore_signal(barrier, inc=1, device_id={"dp": lax.rem(me + o, n)}, device_id_type=MESH)
@@ -113,16 +108,15 @@
 
     def y_copy(t, d, c, ring):
         s = lax.rem(t, SLOTS)
-        return remote(y_cast.at[ring], y_in.at[s, d, c], y_send.at[ring], y_recv.at[s, d, c], z * 2 + 1 - y)
+        return remote(y_cast.at[ring], y_in.at[s, d, c], y_send.at[ring], y_recv.at[d, c], z * 2 + 1 - y)
 
     def s_copy(t, c):
         s = lax.rem(t, SLOTS)
-        h = lax.rem(t, 2)
-        return remote(s_out.at[h, c], s_in.at[s, c], s_send.at[h, c], s_recv.at[s, c], z * 2 + 1 - y)
+        return remote(s_out.at[c], s_in.at[s, c], s_send.at[c], s_recv.at[c], z * 2 + 1 - y)
 
     def z_wait(t, where, c):
         s = lax.rem(t, SLOTS)
-        remote(z_in.at[s, where, c], z_in.at[s, where, c], z_send.at[0, 0], z_recv.at[s, where, c], me).wait_recv()
+        remote(z_in.at[s, where, c], z_in.at[s, where, c], z_send.at[0], z_recv.at[lax.rem(t, 2), where, c], me).wait_recv()
 
     def landed(t, c):
         for k in range(nz - 2):
@@ -147,7 +141,7 @@
         s = lax.rem(t, SLOTS)
         to = jnp.where(is_outer, inner, d)
         where = jnp.where(is_outer, jnp.where(d == inner, d - 1, through(d)), z - 1)
-        remote(src, z_in.at[s, where, c], sem, z_recv.at[s, where, c], to * 2 + y).start()
+        remote(src, z_in.at[s, where, c], sem, z_recv.at[lax.rem(t, 2), where, c], to * 2 + y).start()
 
     def z_sent(sem):
         remote(a_cast.at[0, 0], a_cast.at[0, 0], sem, z_recv.at[0, 0, 0], me).wait_send()
@@ -165,28 +159,26 @@
         y_copy(t, d, c, ring).start()
 
     def s_job(t, c):
-        h = lax.rem(t, 2)
-
-        @pl.when(t >= 2)
+        @pl.when(t > 0)
         def _():
             s_copy(t, c).wait_send()
         j = n_b(z) + (1 - y) * n_a(z) + c
         landed(t, j)
 
         def body(at):
-            s_out[h, c, at, :] = gathered(t, j, at) + mine(t, z, 1 - y, n_b(z) + c, at)
+            s_out[c, at, :] = gathered(t, j, at) + mine(t, z, 1 - y, n_b(z) + c, at)
         loop(body)
         s_copy(t, c).start()
 
-    def a_job(t, i, j):
+    def a_job(t, i, j, gone):
         s = lax.rem(t, SLOTS)
         d = order(i)
         side = j // n_a(d)
         c = n_b(d) + lax.rem(j, n_a(d))
         k = n_b(d) + j
-        sem = z_send.at[i, wide + j]
-
-        @pl.when(t > 0)
+        sem = z_send.at[lax.rem(gone, Z_RING)]
+
+        @pl.when(gone >= Z_RING)
         def _():
             z_sent(sem)
         relay = is_inner & (i > 0)
@@ -208,12 +200,12 @@
             loop(body)
             z_go(t, a_cast.at[i, j], d, k, sem)
 
-    def b_job(t, i, c):
+    def b_job(t, i, c, gone):
         s = lax.rem(t, SLOTS)
         d = order(i)
-        sem = z_send.at[i, c]
-
-        @pl.when(t > 0)
+        sem = z_send.at[lax.rem(gone, Z_RING)]
+
+        @pl.when(gone >= Z_RING)
         def _():
             z_sent(sem)
         y_copy(t, d, c, 0).wait_recv()
@@ -254,8 +246,8 @@
                 grad = whole[:, cols]
                 m_old = scale * qm[t, rows_i, cols].astype(jnp.float32)
                 stored = qv[t, rows_i, cols].astype(jnp.float32)
-                inv = 1.0 / jnp.full((1, lanes), v_exp[t, g], jnp.float32)
-                v_old = v_max[t, g] * jnp.exp(jnp.log(stored) * inv)
+                inv = 1.0 / jnp.full((1, lanes), v_exp[g, t], jnp.float32)
+                v_old = v_max[g, t] * jnp.exp(jnp.log(stored) * inv)
                 m = 0.9 * m_old + 0.1 * grad
                 v = 0.95 * v_old + 0.05 * grad * grad
                 w = par[t, rows_i, cols]
@@ -274,10 +266,13 @@
     def update_a(t, c):
         s = lax.rem(t, SLOTS)
 
+        @pl.when((c == 0) & (t == 0))
+        def _():
+            for copy in ins:
+                copy.wait()
+
         @pl.when(c == 0)
         def _():
-            for copy in in_copies(t):
-                copy.wait()
             stat[t] = jnp.full(stat.shape[1:], -jnp.inf, jnp.float32)
         j = n_b(z) + y * n_a(z) + c
         landed(t, j)
@@ -292,14 +287,25 @@
         update(t, c, lambda at: gathered(t, c, at) + (y_in[s, z, c, at, :] + mine(t, z, y, c, at)))
 
     def stat_copy(t, o):
+        h = lax.rem(t, 2)
         return pltpu.make_async_remote_copy(
-            src_ref=stat.at[t], dst_ref=stat_in.at[t, o], send_sem=st_send.at[t, o], recv_sem=st_recv.at[t, o],
+            src_ref=stat.at[t], dst_ref=stat_in.at[h, o], send_sem=st_send.at[h], recv_sem=st_recv.at[h],
             device_id={"dp": lax.rem(me + o, n)}, device_id_type=MESH)
 
     def peak_copy(t, o):
+        h = lax.rem(t, 2)
         return pltpu.make_async_remote_copy(
-            src_ref=peak.at[t], dst_ref=peak_in.at[t, o], send_sem=pk_send.at[t, o], recv_sem=pk_recv.at[t, o],
+            src_ref=peak.at[t], dst_ref=peak_in.at[h, o], send_sem=pk_send.at[h], recv_sem=pk_recv.at[h],
             device_id={"tensor": lax.rem(mt + o, peers)}, device_id_type=MESH)
+
+    def stats_of(t):
+        h = lax.rem(t, 2)
+        return remote(stat_in.at[h, pl.ds(1, n - 1)], stat_in.at[h, pl.ds(1, n - 1)], st_send.at[h], st_recv.at[h], me)
+
+    def peaks_of(t):
+        h = lax.rem(t, 2)
+        return remote(peak_in.at[h, pl.ds(1, peers - 1)], peak_in.at[h, pl.ds(1, peers - 1)],
+                      pk_send.at[h], pk_recv.at[h], me)
 
     def each(lo, hi, act):
         def one(o, _):
@@ -308,21 +314,34 @@
         lax.fori_loop(lo, hi, one, 0)
 
     def share(t):
-        out_copy(par, out_p, t, 0).start()
+        if isinstance(t, int):
+            if t >= 2:
+                stats_of(t).wait_send()
+        else:
+            @pl.when(t >= 2)
+            def _():
+                stats_of(t).wait_send()
         each(1, n, lambda o: stat_copy(t, o).start())
 
     def all_rows(body):
         def one(i, _):
-            body(pl.ds(pl.multiple_of(i * STEP, STEP), STEP))
+            body(pl.ds(pl.multiple_of(i * LONG, LONG), LONG))
             return 0
-        lax.fori_loop(0, rows // STEP, one, 0)
+        lax.fori_loop(0, rows // LONG, one, 0)
 
     def finish(t):
         h = lax.rem(t, 2)
-        each(1, n, lambda o: stat_copy(t, o).wait_recv())
-        best = lax.fori_loop(1, n, lambda o, b: jnp.maximum(b, stat_in[t, o]), stat[t])
+        stats_of(t).wait_recv()
+        best = lax.fori_loop(1, n, lambda o, b: jnp.maximum(b, stat_in[h, o]), stat[t])
         best = jnp.broadcast_to(jnp.max(best, axis=1, keepdims=True), best.shape)
         peak[t] = best
+        if isinstance(t, int):
+            if t >= 2:
+                peaks_of(t).wait_send()
+        else:
+            @pl.when(t >= 2)
+            def _():
+                peaks_of(t).wait_send()
         each(1, peers, lambda o: peak_copy(t, o).start())
         exps, invs = [], []
         for g in range(groups):
@@ -338,13 +357,13 @@
                 cols = slice(g * lanes, (g + 1) * lanes)
                 value = jnp.exp(exps[g] * jnp.log(v_new[h, at, cols] * invs[g]))
                 qv[t, at, cols] = value.astype(jnp.bfloat16)
-        all_rows(body)
-        out_copy(qv, out_v, t, 1).start()
+        if not isinstance(t, int):
+            all_rows(body)
 
     def scale(t):
         h = lax.rem(t, 2)
-        each(1, peers, lambda o: peak_copy(t, o).wait_recv())
-        whole = lax.fori_loop(1, peers, lambda o, b: jnp.maximum(b, peak_in[t, o]), peak[t])[0:1, :] + 1e-06
+        peaks_of(t).wait_recv()
+        whole = lax.fori_loop(1, peers, lambda o, b: jnp.maximum(b, peak_in[h, o]), peak[t])[0:1, :] + 1e-06
         out_s[t, 0:1, :] = whole
         inverse = 1.0 / whole
 
@@ -352,8 +371,8 @@
             for g in range(groups):
                 cols = slice(g * lanes, (g + 1) * lanes)
                 qm[t, at, cols] = (m_new[h, at, cols] * inverse).astype(jnp.bfloat16)
-        all_rows(body)
-        out_copy(qm, out_m, t, 2).start()
+        if not isinstance(t, int):
+            all_rows(body)
 
     lag_a = jnp.where(is_inner, LAG_A, -LEAD)
     lag_b = jnp.where(is_inner, LAG_B_INNER, LAG_B)
@@ -365,20 +384,25 @@
         g = jnp.clip(g, 0, count * period - 1)
         return ok, g // period, lax.rem(g, period)
 
-    def one(it, sent):
+    def one(it, carry):
+        sent, gone = carry
         g = it - LEAD
         ok, t, p = place(g, -LEAD)
 
-        @pl.when(ok & (p == 0))
-        def _():
-            raw_copy(t).wait()
+        for u, c in enumerate(raws):
+            @pl.when(ok & (p == 0) & (t == u))
+            def _():
+                c.wait()
 
         ok, t, p = place(g, lag_a)
         i, j = jnp.minimum(p // tall, nz - 2), lax.rem(p, tall)
 
-        @pl.when(ok & (p < tall * (nz - 1)) & (j < 2 * n_a(order(i))))
-        def _():
-            a_job(t, i, j)
+        live = ok & (p < tall * (nz - 1)) & (j < 2 * n_a(order(i)))
+
+        @pl.when(live)
+        def _():
+            a_job(t, i, j, gone)
+        gone = gone + jnp.where(live, 1, 0)
 
         ok, t, p = place(g, 0)
         tail = p >= own
@@ -399,9 +423,12 @@
         ok, t, p = place(g, lag_b)
         i, c = p // wide, lax.rem(p, wide)
 
-        @pl.when(ok & (p < own - sides) & (c < n_b(order(i))))
-        def _():
-            b_job(t, i, c)
+        live = ok & (p < own - sides) & (c < n_b(order(i)))
+
+        @pl.when(live)
+        def _():
+            b_job(t, i, c, gone)
+        gone = gone + jnp.where(live, 1, 0)
 
         ok, t, p = place(g, LAG_UPDATE)
         c = p - (own - sides)
@@ -415,42 +442,80 @@
         def _():
             update_b(t, c)
 
+        @pl.when(ok & (p == period - 1) & (t < count - 1))
+        def _():
+            share(t)
+
+        ok, t, p = place(g, LAG_UPDATE + LAG_FINISH)
+
         @pl.when(ok & (p == period - 1))
         def _():
-            share(t)
-
-        ok, t, p = place(g, LAG_UPDATE + LAG_FINISH)
+            finish(t)
+
+        ok, t, p = place(g, LAG_UPDATE + LAG_FINISH + LAG_SCALE)
 
         @pl.when(ok & (p == period - 1))
         def _():
-            finish(t)
-
-        ok, t, p = place(g, LAG_UPDATE + LAG_FINISH + LAG_SCALE)
-
-        @pl.when(ok & (p == period - 1))
-        def _():
             scale(t)
-        return sent
-
-    steps = LEAD + count * period + LAG_UPDATE + LAG_FINISH + LAG_SCALE
-    lax.fori_loop(0, steps, one, 0)
+        return sent, gone
+
+    lax.fori_loop(0, LEAD + count * period + LAG_UPDATE, one, (0, 0))
+    share(count - 1)
+    finish(count - 1)
+    scale(count - 1)
 
     each(0, RING, lambda r: y_copy(0, 0, 0, r).wait_send())
 
-    def drain(i, _):
-        d = order(i)
-        each(0, n_b(d), lambda c: z_sent(z_send.at[i, c]))
-        each(0, 2 * n_a(d), lambda j: z_sent(z_send.at[i, wide + j]))
+    each(0, Z_RING, lambda r: z_sent(z_send.at[r]))
+    each(0, n_a(z), lambda c: s_copy(0, c).wait_send())
+    for t in range(max(0, count - 2), count):
+        stats_of(t).wait_send()
+        peaks_of(t).wait_send()
+
+
+def last(par, qm, qv, m_new, v_new, stats, out_p, out_m, out_v, out_scale, out_top, out_exp,
+         qm_last, qv_last, sem):
+    count, rows, width = par.shape
+    groups = out_top.shape[0]
+    lanes = width // groups
+    t = count - 1
+    h = t % 2
+    copies = [pltpu.make_async_copy(par, out_p, sem.at[0])]
+    for i, (src, dst) in enumerate(((qm, out_m), (qv, out_v))):
+        if count > 1:
+            copies.append(pltpu.make_async_copy(src.at[pl.ds(0, t)], dst.at[pl.ds(0, t)], sem.at[1 + i]))
+    for c in copies:
+        c.start()
+    lane = lax.broadcasted_iota(jnp.int32, (1, lanes), 1)
+
+    def packed(row):
+        line = stats[0, row:row + 1, :]
+        for u in range(1, count):
+            line = jnp.where(lane == u, stats[u, row:row + 1, :], line)
+        return line[:, :count]
+    out_scale[...] = packed(0)
+    for g in range(groups):
+        out_top[g:g + 1, :] = packed(1 + g)
+        out_exp[g:g + 1, :] = packed(1 + groups + g)
+    inverse = 1.0 / stats[t, 0:1, :]
+    invs = [1.0 / stats[t, 1 + g:2 + g, :] for g in range(groups)]
+    exps = [stats[t, 1 + groups + g:2 + groups + g, :] for g in range(groups)]
+
+    def body(i, _):
+        at = pl.ds(pl.multiple_of(i * LONG, LONG), LONG)
+        for g in range(groups):
+            cols = slice(g * lanes, (g + 1) * lanes)
+            value = jnp.exp(exps[g] * jnp.log(v_new[h, at, cols] * invs[g]))
+            qv_last[at, cols] = value.astype(jnp.bfloat16)
+            qm_last[at, cols] = (m_new[h, at, cols] * inverse).astype(jnp.bfloat16)
         return 0
-    lax.fori_loop(0, nz - 1, drain, 0)
-    for t in range(max(0, count - 2), count):
-        each(0, n_a(z), lambda c: s_copy(t, c).wait_send())
-    for t in range(count):
-        each(1, n, lambda o: stat_copy(t, o).wait_send())
-        each(1, peers, lambda o: peak_copy(t, o).wait_send())
-        out_copy(par, out_p, t, 0).wait()
-        out_copy(qv, out_v, t, 1).wait()
-        out_copy(qm, out_m, t, 2).wait()
+    lax.fori_loop(0, rows // LONG, body, 0)
+    for i, (src, dst) in enumerate(((qm_last, out_m), (qv_last, out_v))):
+        c = pltpu.make_async_copy(src, dst.at[t], sem.at[3 + i])
+        c.start()
+        copies.append(c)
+    for c in copies:
+        c.wait()
 
 
 def on_device(n, peers, grads, param, q_m, m_scale, q_v, v_max, v_exp):
@@ -465,48 +530,64 @@
     dma = pltpu.SemaphoreType.DMA
     hbm = pl.BlockSpec(memory_space=pl.ANY)
     smem = pl.BlockSpec(memory_space=pltpu.SMEM)
-    new_param, new_q_m, new_q_v, stats = pl.pallas_call(
+    vmem = pl.BlockSpec(memory_space=pltpu.VMEM)
+    buffers = [
+        pltpu.VMEM((count, n, rows, width), bf16),
+        pltpu.VMEM((RING, chunk, width), f32),
+        pltpu.VMEM((nz - 1, tall, chunk, width), f32),
+        pltpu.VMEM((SLOTS, nz, wide, chunk, width), f32),
+        pltpu.VMEM((SLOTS, 2 * (nz - 2), deep, chunk, width), f32),
+        pltpu.VMEM((2 * SPLIT, chunk, width), f32),
+        pltpu.VMEM((SLOTS, 2 * SPLIT, chunk, width), f32),
+        pltpu.VMEM((count, kinds, lanes), f32),
+        pltpu.VMEM((2, n, kinds, lanes), f32),
+        pltpu.VMEM((count, kinds, lanes), f32),
+        pltpu.VMEM((2, peers, kinds, lanes), f32),
+    ]
+    grant = SPARE + sum(math.prod(b.shape) * b.dtype.itemsize for b in buffers)
+    state = pl.pallas_call(
         functools.partial(kernel, n, peers),
         out_shape=(
-            jax.ShapeDtypeStruct(param.shape, f32),
-            jax.ShapeDtypeStruct(q_m.shape, bf16),
-            jax.ShapeDtypeStruct(q_v.shape, bf16),
-            jax.ShapeDtypeStruct((count, kinds, lanes), f32),
-        ),
-        in_specs=[hbm] * 4 + [smem] * 3,
-        out_specs=(hbm, hbm, hbm, pl.BlockSpec(memory_space=pltpu.VMEM)),
-        scratch_shapes=[
-            pltpu.VMEM((count, n, rows, width), bf16),
-            pltpu.VMEM((RING, chunk, width), f32),
-            pltpu.VMEM((nz - 1, tall, chunk, width), f32),
-            pltpu.VMEM((SLOTS, nz, wide, chunk, width), f32),
-            pltpu.VMEM((SLOTS, 2 * (nz - 2), deep, chunk, width), f32),
-            pltpu.VMEM((2, 2 * SPLIT, chunk, width), f32),
-            pltpu.VMEM((SLOTS, 2 * SPLIT, chunk, width), f32),
             pltpu.VMEM(param.shape, f32),
             pltpu.VMEM(q_m.shape, bf16),
             pltpu.VMEM(q_v.shape, bf16),
             pltpu.VMEM((2, rows, width), f32),
             pltpu.VMEM((2, rows, width), f32),
             pltpu.VMEM((count, kinds, lanes), f32),
-            pltpu.VMEM((count, n, kinds, lanes), f32),
-            pltpu.VMEM((count, kinds, lanes), f32),
-            pltpu.VMEM((count, peers, kinds, lanes), f32),
-            dma((count,)), dma((count, 3)), dma((count, 3)),
-            dma((RING,)), dma((SLOTS, nz, wide)),
-            dma((nz - 1, wide + tall)), dma((SLOTS, 2 * (nz - 2), deep)),
-            dma((2, 2 * SPLIT)), dma((SLOTS, 2 * SPLIT)),
-            dma((count, n)), dma((count, n)),
-            dma((count, peers)), dma((count, peers)),
+        ),
+        in_specs=[hbm] * 4 + [smem] * 3,
+        out_specs=[vmem] * 6,
+        scratch_shapes=buffers + [
+            dma((2,)), dma((3,)),
+            dma((RING,)), dma((nz, wide)),
+            dma((Z_RING,)), dma((2, 2 * (nz - 2), deep)),
+            dma((2 * SPLIT,)), dma((2 * SPLIT,)),
+            dma((2,)), dma((2,)), dma((2,)), dma((2,)),
         ],
         compiler_params=pltpu.CompilerParams(
-            collective_id=0, has_side_effects=True, vmem_limit_bytes=67043328
+            collective_id=0, has_side_effects=True, vmem_limit_bytes=grant
         ),
-    )(grads[0].reshape(count, n, rows, width), param, q_m, q_v, m_scale, v_max, v_exp)
-    new_m_scale = stats[:, 0, 0]
-    group_top = stats[:, 1:1 + groups, 0]
-    new_v_exp = stats[:, 1 + groups:1 + 2 * groups, 0]
-    return new_param, new_q_m, new_m_scale, new_q_v, group_top, new_v_exp
+    )(grads[0].reshape(count, n, rows, width), param, q_m, q_v, m_scale, v_max.T, v_exp.T)
+    new_param, new_q_m, new_q_v, scales, tops, exps = pl.pallas_call(
+        last,
+        out_shape=(
+            jax.ShapeDtypeStruct(param.shape, f32),
+            jax.ShapeDtypeStruct(q_m.shape, bf16),
+            jax.ShapeDtypeStruct(q_v.shape, bf16),
+            jax.ShapeDtypeStruct((1, count), f32),
+            jax.ShapeDtypeStruct((groups, count), f32),
+            jax.ShapeDtypeStruct((groups, count), f32),
+        ),
+        in_specs=[vmem] * 6,
+        out_specs=[hbm] * 3 + [vmem] * 3,
+        scratch_shapes=[
+            pltpu.VMEM((rows, width), bf16),
+            pltpu.VMEM((rows, width), bf16),
+            dma((5,)),
+        ],
+        compiler_params=pltpu.CompilerParams(vmem_limit_bytes=4 << 20),
+    )(*state)
+    return new_param, new_q_m, scales.reshape(count), new_q_v, tops.T, exps.T
 
 
 def solution(mesh):

time: 359 us -> 339 us (0.944)
  local copies, waits for them, and re-layouts: 14.5 us -> 0 us
  Pallas kernels: 343 us -> 338 us
    unnamed x9 -> x0, local copies, waits for them, and re-layouts: 11.1 us -> none
    pallas_call x1 -> x2, Pallas kernels: 343 us -> 338 us  [the longest x1 334 us: on_device(): pl.pallas_call(functools.partial(kernel, n, peers), out_shape=(pltpu.VMEM...]
where the time goes in v2:
time: 339 us; the launch traced here: 338 us
  Pallas kernels  338 us (100%)
    pallas_call x1, Pallas kernels, on_device(): pl.pallas_call(functools.partial(kernel, n, peers), out_shape=(pltpu.VMEM...  334 us

profile of v2, /device:TPU:0, one launch (start us, length us, event | category | flops | bytes accessed | tf_op | source)
XLA Modules:
  0.0 338.3 jit_solution(3362975108977294248)
XLA Ops:
  0.6 333.8 %shard_map.118 = (f32[4,1024,256]{2,1,0:T(8,128)S(1)}, bf16[4,1024,256]{2,1,0:T(8,128)(2,1)S(1)}, bf16[4,1024,256]{2,1,0:T(8,128)(2,1)S(1)}, f32[2,1024,256]{2,1...) custom-call(bf16[4,8,1024,256]{3,2,1,0:T(8,128)(2,1)} %bitcast.6, f32[4,1024,256]{2,1,0:T(8,128)} %refs_1_.1, ...), custom_call_target="tpu_custom_call" | custom-call | tf_op jit(solution)/shard_map/pallas_call | solution.py:548
  334.4 3.9 %shard_map.119 = (f32[4,1024,256]{2,1,0:T(8,128)}, bf16[4,1024,256]{2,1,0:T(8,128)(2,1)}, bf16[4,1024,256]{2,1,0:T(8,128)(2,1)}, f32[1,4]{1,0:T(1,128)}, f32[2,4]{1,0:T(2,128)}, /*index=5*/f32[2,4]{1,0:T(2,128)}) custom-call(f32[4,1024,256]{2,1,0:T(8,128)S(1)} %get-tuple-element.18.par, bf16[4,1024,256]{2,1,0:T(8,128)(2,1)S(1)} %get-tuple-element.19.qm, ...), custom_call_target="tpu_custom_call" | custom-call | tf_op jit(solution)/shard_map/pallas_call | solution.py:571

commit v3 on v2

--- a/solution.py
+++ b/solution.py
@@ -21,17 +21,36 @@
 LAG_B_INNER = 9
 LAG_UPDATE = 5
 LAG_FINISH = 10
-LAG_SCALE = 5
 SPARE = 1 << 20
+
+
+def merged(n, groups, row, row_in, out, t, h):
+    lane = lax.broadcasted_iota(jnp.int32, row.shape[1:], 1)
+
+    def pick(line, k):
+        return jnp.broadcast_to(jnp.max(jnp.where(lane == k, line, -jnp.inf), axis=1, keepdims=True), line.shape)
+    best = jnp.maximum(row[h], jnp.max(row_in[h, pl.ds(1, n - 1)], axis=0))
+    every = jnp.maximum(best, jnp.max(row_in[h, pl.ds(n, row_in.shape[1] - n)], axis=0))
+    whole = pick(every, 0) + 1e-06
+    out[t, 0:1, :] = whole
+    exps, invs = [], []
+    for g in range(groups):
+        top = pick(best, 1 + g)
+        low = -pick(best, 1 + groups + g)
+        exps.append(12.343 / jnp.maximum(jnp.log(top / low), 1.0))
+        invs.append(1.0 / top)
+        out[t, 1 + g:2 + g, :] = top
+        out[t, 1 + groups + g:2 + groups + g, :] = exps[g]
+    return 1.0 / whole, exps, invs
 
 
 def kernel(n, peers, *refs):
     (grads, param, q_m, q_v, m_scale, v_max, v_exp,
-     par, qm, qv, m_new, v_new, out_s,
+     par, qm, qv, m_new, v_new, out_s, row, row_in,
      raw, y_cast, a_cast, y_in, z_in, s_out, s_in,
-     stat, stat_in, peak, peak_in,
-     raw_sem, in_sem, y_send, y_recv, z_send, z_recv, s_send, s_recv,
-     st_send, st_recv, pk_send, pk_recv) = refs
+     stat,
+     first_sem, rest_sem, y_send, y_recv, z_send, z_recv, s_send, s_recv,
+     st_send, st_recv) = refs
     count, _, rows, width = grads.shape
     groups = v_max.shape[0]
     lanes = width // groups
@@ -74,23 +93,33 @@
 
     barrier = pltpu.get_barrier_semaphore()
 
-    raws = [pltpu.make_async_copy(grads.at[at], raw.at[at], raw_sem.at[i])
-            for i, at in enumerate((pl.ds(0, 1), pl.ds(1, count - 1)))]
-    ins = [pltpu.make_async_copy(src, dst, in_sem.at[i])
-           for i, (src, dst) in enumerate(((q_m, qm), (q_v, qv), (param, par)))]
-    for c in raws + ins:
-        c.start()
-
-    def greet(o, _):
-        pl.semaphore_signal(barrier, inc=1, device_id={"dp": lax.rem(me + o, n)}, device_id_type=MESH)
-        return 0
-    lax.fori_loop(1, n, greet, 0)
-
-    def greet_t(o, _):
-        pl.semaphore_signal(barrier, inc=1, device_id={"tensor": lax.rem(mt + o, peers)}, device_id_type=MESH)
-        return 0
-    lax.fori_loop(1, peers, greet_t, 0)
-    pl.semaphore_wait(barrier, n - 1 + peers - 1)
+    def first_copy(i):
+        at = pl.ds(order(i) * 2, 2)
+        return pltpu.make_async_copy(grads.at[0, at], raw.at[0, at], first_sem.at[i])
+
+    later = pl.ds(1, count - 1)
+    rest = [pltpu.make_async_copy(src, dst, rest_sem.at[i]) for i, (src, dst) in enumerate((
+        (grads.at[later], raw.at[later]), (q_m, qm), (q_v, qv), (param, par)))]
+    first_copy(0).start()
+
+    def each(lo, hi, act):
+        def one(o, _):
+            act(o)
+            return 0
+        lax.fori_loop(lo, hi, one, 0)
+
+    def greet(axis, to):
+        pl.semaphore_signal(barrier, inc=1, device_id={axis: to}, device_id_type=MESH)
+
+    def greet_z(o):
+        @pl.when(jnp.logical_not(is_outer & ((z + o == nz - 1) | (z + o == nz))))
+        def _():
+            greet("dp", lax.rem(z + o, nz) * 2 + y)
+    greet("dp", z * 2 + 1 - y)
+    each(1, nz, greet_z)
+    each(1, peers, lambda o: greet("tensor", lax.rem(mt + o, peers)))
+    each(1, nz, lambda i: first_copy(i).start())
+    pl.semaphore_wait(barrier, nz - 1 + jnp.minimum(zm, 1) + peers - 1)
 
     def remote(src, dst, s_sem, r_sem, to):
         return pltpu.make_async_remote_copy(src_ref=src, dst_ref=dst, send_sem=s_sem, recv_sem=r_sem,
@@ -268,7 +297,7 @@
 
         @pl.when((c == 0) & (t == 0))
         def _():
-            for copy in ins:
+            for copy in rest[1:]:
                 copy.wait()
 
         @pl.when(c == 0)
@@ -286,42 +315,30 @@
         landed(t, c)
         update(t, c, lambda at: gathered(t, c, at) + (y_in[s, z, c, at, :] + mine(t, z, y, c, at)))
 
-    def stat_copy(t, o):
+    def row_copy(t, o):
         h = lax.rem(t, 2)
         return pltpu.make_async_remote_copy(
-            src_ref=stat.at[t], dst_ref=stat_in.at[h, o], send_sem=st_send.at[h], recv_sem=st_recv.at[h],
-            device_id={"dp": lax.rem(me + o, n)}, device_id_type=MESH)
-
-    def peak_copy(t, o):
+            src_ref=row.at[h], dst_ref=row_in.at[h, o], send_sem=st_send.at[h], recv_sem=st_recv.at[h],
+            device_id={"tensor": lax.rem(mt + o // n, peers), "dp": lax.rem(me + lax.rem(o, n), n)},
+            device_id_type=MESH)
+
+    def rows_of(t):
         h = lax.rem(t, 2)
-        return pltpu.make_async_remote_copy(
-            src_ref=peak.at[t], dst_ref=peak_in.at[h, o], send_sem=pk_send.at[h], recv_sem=pk_recv.at[h],
-            device_id={"tensor": lax.rem(mt + o, peers)}, device_id_type=MESH)
-
-    def stats_of(t):
+        part = row_in.at[h, pl.ds(1, n * peers - 1)]
+        return remote(part, part, st_send.at[h], st_recv.at[h], me)
+
+    kinds = stat.shape[1]
+
+    def share(t):
         h = lax.rem(t, 2)
-        return remote(stat_in.at[h, pl.ds(1, n - 1)], stat_in.at[h, pl.ds(1, n - 1)], st_send.at[h], st_recv.at[h], me)
-
-    def peaks_of(t):
-        h = lax.rem(t, 2)
-        return remote(peak_in.at[h, pl.ds(1, peers - 1)], peak_in.at[h, pl.ds(1, peers - 1)],
-                      pk_send.at[h], pk_recv.at[h], me)
-
-    def each(lo, hi, act):
-        def one(o, _):
-            act(o)
-            return 0
-        lax.fori_loop(lo, hi, one, 0)
-
-    def share(t):
-        if isinstance(t, int):
-            if t >= 2:
-                stats_of(t).wait_send()
-        else:
+        if not isinstance(t, int) or t >= 2:
             @pl.when(t >= 2)
             def _():
-                stats_of(t).wait_send()
-        each(1, n, lambda o: stat_copy(t, o).start())
+                rows_of(t).wait_send()
+        best = jnp.broadcast_to(jnp.max(stat[t], axis=1, keepdims=True), (kinds, lanes))
+        at = [lax.broadcasted_iota(jnp.int32, (kinds, lanes), i) for i in range(2)]
+        row[h] = jnp.max(jnp.where(at[0] == at[1], best, -jnp.inf), axis=0, keepdims=True)
+        each(1, n * peers, lambda o: row_copy(t, o).start())
 
     def all_rows(body):
         def one(i, _):
@@ -331,48 +348,16 @@
 
     def finish(t):
         h = lax.rem(t, 2)
-        stats_of(t).wait_recv()
-        best = lax.fori_loop(1, n, lambda o, b: jnp.maximum(b, stat_in[h, o]), stat[t])
-        best = jnp.broadcast_to(jnp.max(best, axis=1, keepdims=True), best.shape)
-        peak[t] = best
-        if isinstance(t, int):
-            if t >= 2:
-                peaks_of(t).wait_send()
-        else:
-            @pl.when(t >= 2)
-            def _():
-                peaks_of(t).wait_send()
-        each(1, peers, lambda o: peak_copy(t, o).start())
-        exps, invs = [], []
-        for g in range(groups):
-            top = best[1 + g:2 + g, :]
-            low = -best[1 + groups + g:2 + groups + g, :]
-            exps.append(12.343 / jnp.maximum(jnp.log(top / low), 1.0))
-            invs.append(1.0 / top)
-            out_s[t, 1 + g:2 + g, :] = top
-            out_s[t, 1 + groups + g:2 + groups + g, :] = exps[g]
+        rows_of(t).wait_recv()
+        inverse, exps, invs = merged(n, groups, row, row_in, out_s, t, h)
 
         def body(at):
             for g in range(groups):
                 cols = slice(g * lanes, (g + 1) * lanes)
                 value = jnp.exp(exps[g] * jnp.log(v_new[h, at, cols] * invs[g]))
                 qv[t, at, cols] = value.astype(jnp.bfloat16)
-        if not isinstance(t, int):
-            all_rows(body)
-
-    def scale(t):
-        h = lax.rem(t, 2)
-        peaks_of(t).wait_recv()
-        whole = lax.fori_loop(1, peers, lambda o, b: jnp.maximum(b, peak_in[h, o]), peak[t])[0:1, :] + 1e-06
-        out_s[t, 0:1, :] = whole
-        inverse = 1.0 / whole
-
-        def body(at):
-            for g in range(groups):
-                cols = slice(g * lanes, (g + 1) * lanes)
                 qm[t, at, cols] = (m_new[h, at, cols] * inverse).astype(jnp.bfloat16)
-        if not isinstance(t, int):
-            all_rows(body)
+        all_rows(body)
 
     lag_a = jnp.where(is_inner, LAG_A, -LEAD)
     lag_b = jnp.where(is_inner, LAG_B_INNER, LAG_B)
@@ -389,10 +374,19 @@
         g = it - LEAD
         ok, t, p = place(g, -LEAD)
 
-        for u, c in enumerate(raws):
-            @pl.when(ok & (p == 0) & (t == u))
-            def _():
-                c.wait()
+        @pl.when(ok & (t == 0) & (p == 0))
+        def _():
+            first_copy(0).wait()
+
+        @pl.when(ok & (t == 0) & (p == LEAD + 2))
+        def _():
+            for c in rest:
+                c.start()
+            each(1, nz, lambda i: first_copy(i).wait())
+
+        @pl.when(ok & (t == 1) & (p == 0))
+        def _():
+            rest[0].wait()
 
         ok, t, p = place(g, lag_a)
         i, j = jnp.minimum(p // tall, nz - 2), lax.rem(p, tall)
@@ -451,30 +445,22 @@
         @pl.when(ok & (p == period - 1))
         def _():
             finish(t)
-
-        ok, t, p = place(g, LAG_UPDATE + LAG_FINISH + LAG_SCALE)
-
-        @pl.when(ok & (p == period - 1))
-        def _():
-            scale(t)
         return sent, gone
 
     lax.fori_loop(0, LEAD + count * period + LAG_UPDATE, one, (0, 0))
     share(count - 1)
-    finish(count - 1)
-    scale(count - 1)
+    rows_of(count - 1).wait_recv()
 
     each(0, RING, lambda r: y_copy(0, 0, 0, r).wait_send())
 
     each(0, Z_RING, lambda r: z_sent(z_send.at[r]))
     each(0, n_a(z), lambda c: s_copy(0, c).wait_send())
     for t in range(max(0, count - 2), count):
-        stats_of(t).wait_send()
-        peaks_of(t).wait_send()
-
-
-def last(par, qm, qv, m_new, v_new, stats, out_p, out_m, out_v, out_scale, out_top, out_exp,
-         qm_last, qv_last, sem):
+        rows_of(t).wait_send()
+
+
+def last(n, par, qm, qv, m_new, v_new, old, row, row_in, out_p, out_m, out_v, out_scale, out_top, out_exp,
+         qm_last, qv_last, stats, scale, top, exp, sem):
     count, rows, width = par.shape
     groups = out_top.shape[0]
     lanes = width // groups
@@ -482,24 +468,26 @@
     h = t % 2
     copies = [pltpu.make_async_copy(par, out_p, sem.at[0])]
     for i, (src, dst) in enumerate(((qm, out_m), (qv, out_v))):
-        if count > 1:
-            copies.append(pltpu.make_async_copy(src.at[pl.ds(0, t)], dst.at[pl.ds(0, t)], sem.at[1 + i]))
+        copies.append(pltpu.make_async_copy(src.at[pl.ds(0, t)], dst.at[pl.ds(0, t)], sem.at[1 + i]))
     for c in copies:
         c.start()
+    stats[pl.ds(0, t)] = old[pl.ds(0, t)]
+    inverse, exps, invs = merged(n, groups, row, row_in, stats, t, h)
     lane = lax.broadcasted_iota(jnp.int32, (1, lanes), 1)
 
-    def packed(row):
-        line = stats[0, row:row + 1, :]
+    def packed(k):
+        line = stats[0, k:k + 1, :]
         for u in range(1, count):
-            line = jnp.where(lane == u, stats[u, row:row + 1, :], line)
+            line = jnp.where(lane == u, stats[u, k:k + 1, :], line)
         return line[:, :count]
-    out_scale[...] = packed(0)
+    scale[...] = packed(0)
     for g in range(groups):
-        out_top[g:g + 1, :] = packed(1 + g)
-        out_exp[g:g + 1, :] = packed(1 + groups + g)
-    inverse = 1.0 / stats[t, 0:1, :]
-    invs = [1.0 / stats[t, 1 + g:2 + g, :] for g in range(groups)]
-    exps = [stats[t, 1 + groups + g:2 + groups + g, :] for g in range(groups)]
+        top[g:g + 1, :] = packed(1 + g)
+        exp[g:g + 1, :] = packed(1 + groups + g)
+    for i, (src, dst) in enumerate(((scale, out_scale), (top, out_top), (exp, out_exp))):
+        c = pltpu.make_async_copy(src, dst, sem.at[3 + i])
+        c.start()
+        copies.append(c)
 
     def body(i, _):
         at = pl.ds(pl.multiple_of(i * LONG, LONG), LONG)
@@ -511,7 +499,7 @@
         return 0
     lax.fori_loop(0, rows // LONG, body, 0)
     for i, (src, dst) in enumerate(((qm_last, out_m), (qv_last, out_v))):
-        c = pltpu.make_async_copy(src, dst.at[t], sem.at[3 + i])
+        c = pltpu.make_async_copy(src, dst.at[t], sem.at[6 + i])
         c.start()
         copies.append(c)
     for c in copies:
@@ -540,9 +528,6 @@
         pltpu.VMEM((2 * SPLIT, chunk, width), f32),
         pltpu.VMEM((SLOTS, 2 * SPLIT, chunk, width), f32),
         pltpu.VMEM((count, kinds, lanes), f32),
-        pltpu.VMEM((2, n, kinds, lanes), f32),
-        pltpu.VMEM((count, kinds, lanes), f32),
-        pltpu.VMEM((2, peers, kinds, lanes), f32),
     ]
     grant = SPARE + sum(math.prod(b.shape) * b.dtype.itemsize for b in buffers)
     state = pl.pallas_call(
@@ -554,22 +539,24 @@
             pltpu.VMEM((2, rows, width), f32),
             pltpu.VMEM((2, rows, width), f32),
             pltpu.VMEM((count, kinds, lanes), f32),
+            pltpu.VMEM((2, 1, lanes), f32),
+            pltpu.VMEM((2, n * peers, 1, lanes), f32),
         ),
         in_specs=[hbm] * 4 + [smem] * 3,
-        out_specs=[vmem] * 6,
+        out_specs=[vmem] * 8,
         scratch_shapes=buffers + [
-            dma((2,)), dma((3,)),
+            dma((nz,)), dma((4,)),
             dma((RING,)), dma((nz, wide)),
             dma((Z_RING,)), dma((2, 2 * (nz - 2), deep)),
             dma((2 * SPLIT,)), dma((2 * SPLIT,)),
-            dma((2,)), dma((2,)), dma((2,)), dma((2,)),
+            dma((2,)), dma((2,)),
         ],
         compiler_params=pltpu.CompilerParams(
             collective_id=0, has_side_effects=True, vmem_limit_bytes=grant
         ),
     )(grads[0].reshape(count, n, rows, width), param, q_m, q_v, m_scale, v_max.T, v_exp.T)
     new_param, new_q_m, new_q_v, scales, tops, exps = pl.pallas_call(
-        last,
+        functools.partial(last, n),
         out_shape=(
             jax.ShapeDtypeStruct(param.shape, f32),
             jax.ShapeDtypeStruct(q_m.shape, bf16),
@@ -578,12 +565,16 @@
             jax.ShapeDtypeStruct((groups, count), f32),
             jax.ShapeDtypeStruct((groups, count), f32),
         ),
-        in_specs=[vmem] * 6,
-        out_specs=[hbm] * 3 + [vmem] * 3,
+        in_specs=[vmem] * 8,
+        out_specs=[hbm] * 6,
         scratch_shapes=[
             pltpu.VMEM((rows, width), bf16),
             pltpu.VMEM((rows, width), bf16),
-            dma((5,)),
+            pltpu.VMEM((count, kinds, lanes), f32),
+            pltpu.VMEM((1, count), f32),
+            pltpu.VMEM((groups, count), f32),
+            pltpu.VMEM((groups, count), f32),
+            dma((8,)),
         ],
         compiler_params=pltpu.CompilerParams(vmem_limit_bytes=4 << 20),
     )(*state)

time: 339 us -> 334 us (0.985)
  Pallas kernels: 338 us -> 333 us
    pallas_call x1, Pallas kernels: 334 us -> 330 us  [on_device(): pl.pallas_call(functools.partial(kernel, n, peers), out_shape=(pltpu.VMEM...]
where the time goes in v3:
time: 334 us
  Pallas kernels  333 us (100%)
    pallas_call x1, Pallas kernels, on_device(): pl.pallas_call(functools.partial(kernel, n, peers), out_shape=(pltpu.VMEM...  330 us

profile of v3, /device:TPU:0, one launch (start us, length us, event | category | flops | bytes accessed | tf_op | source)
XLA Modules:
  0.0 333.7 jit_solution(14460369448795422288)
XLA Ops:
  0.6 329.7 %shard_map.118 = (f32[4,1024,256]{2,1,0:T(8,128)S(1)}, bf16[4,1024,256]{2,1,0:T(8,128)(2,1)S(1)}, bf16[4,1024,256]{2,1,0:T(8,128)(2,1)S(1)}, f32[2,1024,256]{2,1...) custom-call(bf16[4,8,1024,256]{3,2,1,0:T(8,128)(2,1)} %bitcast.6, ...), custom_call_target="tpu_custom_call" | custom-call | tf_op jit(solution)/shard_map/pallas_call | solution.py:533
  330.3 3.4 %shard_map.119 = (f32[4,1024,256]{2,1,0:T(8,128)}, bf16[4,1024,256]{2,1,0:T(8,128)(2,1)}, bf16[4,1024,256]{2,1,0:T(8,128)(2,1)}, f32[1,4]{1,0:T(1,128)}, f32[2,4]{1,0:T(2,128)}, /*index=5*/f32[2,4]{1,0:T(2,128)}) custom-call(f32[4,1024,256]{2,1,0:T(8,128)S(1)} %get-tuple-element.20.par, bf16[4,1024,256]{2,1,0:T(8,128)(2,1)S(1)} %get-tuple-element.21.qm, ...), custom_call_target="tpu_custom_call" | custom-call | tf_op jit(solution)/shard_map/pallas_call | solution.py:558

commit v4 on v3

--- a/solution.py
+++ b/solution.py
@@ -15,7 +15,8 @@
 SLOTS = 3
 RING = 4
 Z_RING = 16
-LEAD = 1
+LEAD = 0
+CHAIN_AT = 3
 LAG_A = 4
 LAG_B = 5
 LAG_B_INNER = 9
@@ -49,7 +50,7 @@
      par, qm, qv, m_new, v_new, out_s, row, row_in,
      raw, y_cast, a_cast, y_in, z_in, s_out, s_in,
      stat,
-     first_sem, rest_sem, y_send, y_recv, z_send, z_recv, s_send, s_recv,
+     first_sem, rest_sem, token, y_send, y_recv, z_send, z_recv, s_send, s_recv,
      st_send, st_recv) = refs
     count, _, rows, width = grads.shape
     groups = v_max.shape[0]
@@ -93,14 +94,15 @@
 
     barrier = pltpu.get_barrier_semaphore()
 
-    def first_copy(i):
-        at = pl.ds(order(i) * 2, 2)
-        return pltpu.make_async_copy(grads.at[0, at], raw.at[0, at], first_sem.at[i])
+    def first_copy(i, lo=0, sem=None):
+        at = (0, pl.ds(order(i) * 2, 2), pl.ds(lo, chunk if sem is not None else rows - lo))
+        return pltpu.make_async_copy(grads.at[at], raw.at[at], first_sem.at[i if sem is None else sem])
 
     later = pl.ds(1, count - 1)
     rest = [pltpu.make_async_copy(src, dst, rest_sem.at[i]) for i, (src, dst) in enumerate((
         (grads.at[later], raw.at[later]), (q_m, qm), (q_v, qv), (param, par)))]
-    first_copy(0).start()
+    first_copy(0, 0, nz).start()
+    first_copy(0, chunk).start()
 
     def each(lo, hi, act):
         def one(o, _):
@@ -111,15 +113,51 @@
     def greet(axis, to):
         pl.semaphore_signal(barrier, inc=1, device_id={axis: to}, device_id_type=MESH)
 
-    def greet_z(o):
-        @pl.when(jnp.logical_not(is_outer & ((z + o == nz - 1) | (z + o == nz))))
-        def _():
-            greet("dp", lax.rem(z + o, nz) * 2 + y)
+    def beside(step):
+        return {"dp": (z + step) * 2 + y}
+    first, final = z == 0, z == nz - 1
     greet("dp", z * 2 + 1 - y)
-    each(1, nz, greet_z)
+
+    @pl.when(jnp.logical_not(first))
+    def _():
+        greet("dp", (z - 1) * 2 + y)
+
+    @pl.when(jnp.logical_not(final))
+    def _():
+        greet("dp", (z + 1) * 2 + y)
     each(1, peers, lambda o: greet("tensor", lax.rem(mt + o, peers)))
     each(1, nz, lambda i: first_copy(i).start())
-    pl.semaphore_wait(barrier, nz - 1 + jnp.minimum(zm, 1) + peers - 1)
+    pl.semaphore_wait(barrier, peers + 2 - jnp.where(first | final, 1, 0))
+
+    def tell(side, step):
+        pl.semaphore_signal(token.at[side], inc=1, device_id=beside(step), device_id_type=MESH)
+
+    def chain():
+        @pl.when(first)
+        def _():
+            tell(0, 1)
+
+        @pl.when(final)
+        def _():
+            tell(1, -1)
+
+        @pl.when(jnp.logical_not(first))
+        def _():
+            pl.semaphore_wait(token.at[0], 1)
+
+            @pl.when(jnp.logical_not(final))
+            def _():
+                tell(0, 1)
+
+        @pl.when(jnp.logical_not(final))
+        def _():
+            pl.semaphore_wait(token.at[1], 1)
+
+            @pl.when(jnp.logical_not(first))
+            def _():
+                tell(1, -1)
+    if nz > 4:
+        chain()
 
     def remote(src, dst, s_sem, r_sem, to):
         return pltpu.make_async_remote_copy(src_ref=src, dst_ref=dst, send_sem=s_sem, recv_sem=r_sem,
@@ -338,7 +376,7 @@
         best = jnp.broadcast_to(jnp.max(stat[t], axis=1, keepdims=True), (kinds, lanes))
         at = [lax.broadcasted_iota(jnp.int32, (kinds, lanes), i) for i in range(2)]
         row[h] = jnp.max(jnp.where(at[0] == at[1], best, -jnp.inf), axis=0, keepdims=True)
-        each(1, n * peers, lambda o: row_copy(t, o).start())
+        each(1, n * peers, lambda o: row_copy(t, n * peers - o).start())
 
     def all_rows(body):
         def one(i, _):
@@ -376,7 +414,7 @@
 
         @pl.when(ok & (t == 0) & (p == 0))
         def _():
-            first_copy(0).wait()
+            first_copy(0, 0, nz).wait()
 
         @pl.when(ok & (t == 0) & (p == LEAD + 2))
         def _():
@@ -384,19 +422,14 @@
                 c.start()
             each(1, nz, lambda i: first_copy(i).wait())
 
+        if nz == 4:
+            @pl.when(g == CHAIN_AT)
+            def _():
+                chain()
+
         @pl.when(ok & (t == 1) & (p == 0))
         def _():
             rest[0].wait()
-
-        ok, t, p = place(g, lag_a)
-        i, j = jnp.minimum(p // tall, nz - 2), lax.rem(p, tall)
-
-        live = ok & (p < tall * (nz - 1)) & (j < 2 * n_a(order(i)))
-
-        @pl.when(live)
-        def _():
-            a_job(t, i, j, gone)
-        gone = gone + jnp.where(live, 1, 0)
 
         ok, t, p = place(g, 0)
         tail = p >= own
@@ -414,6 +447,20 @@
         def _():
             s_job(t, c)
 
+        @pl.when(g == 0)
+        def _():
+            first_copy(0, chunk).wait()
+
+        ok, t, p = place(g, lag_a)
+        i, j = jnp.minimum(p // tall, nz - 2), lax.rem(p, tall)
+
+        live = ok & (p < tall * (nz - 1)) & (j < 2 * n_a(order(i)))
+
+        @pl.when(live)
+        def _():
+            a_job(t, i, j, gone)
+        gone = gone + jnp.where(live, 1, 0)
+
         ok, t, p = place(g, lag_b)
         i, c = p // wide, lax.rem(p, wide)
 
@@ -449,14 +496,13 @@
 
     lax.fori_loop(0, LEAD + count * period + LAG_UPDATE, one, (0, 0))
     share(count - 1)
-    rows_of(count - 1).wait_recv()
 
     each(0, RING, lambda r: y_copy(0, 0, 0, r).wait_send())
-
     each(0, Z_RING, lambda r: z_sent(z_send.at[r]))
     each(0, n_a(z), lambda c: s_copy(0, c).wait_send())
     for t in range(max(0, count - 2), count):
         rows_of(t).wait_send()
+    rows_of(count - 1).wait_recv()
 
 
 def last(n, par, qm, qv, m_new, v_new, old, row, row_in, out_p, out_m, out_v, out_scale, out_top, out_exp,
@@ -545,7 +591,7 @@
         in_specs=[hbm] * 4 + [smem] * 3,
         out_specs=[vmem] * 8,
         scratch_shapes=buffers + [
-            dma((nz,)), dma((4,)),
+            dma((nz + 1,)), dma((4,)), pltpu.SemaphoreType.REGULAR((2,)),
             dma((RING,)), dma((nz, wide)),
             dma((Z_RING,)), dma((2, 2 * (nz - 2), deep)),
             dma((2 * SPLIT,)), dma((2 * SPLIT,)),

time: 334 us -> 333 us (level)
  no operation moved by 1% of the time
where the time goes in v4:
time: 333 us
  Pallas kernels  333 us (100%)
    pallas_call x1, Pallas kernels, on_device(): pl.pallas_call(functools.partial(kernel, n, peers), out_shape=(pltpu.VMEM...  329 us

profile of v4, /device:TPU:0, one launch (start us, length us, event | category | flops | bytes accessed | tf_op | source)
XLA Modules:
  0.0 333.2 jit_solution(6769956671568821790)
XLA Ops:
  0.6 329.2 %shard_map.118 = (f32[4,1024,256]{2,1,0:T(8,128)S(1)}, bf16[4,1024,256]{2,1,0:T(8,128)(2,1)S(1)}, bf16[4,1024,256]{2,1,0:T(8,128)(2,1)S(1)}, f32[2,1024,256]{2,1...) custom-call(bf16[4,8,1024,256]{3,2,1,0:T(8,128)(2,1)} %bitcast.6, ...), custom_call_target="tpu_custom_call" | custom-call | tf_op jit(solution)/shard_map/pallas_call | solution.py:579
  329.8 3.4 %shard_map.119 = (f32[4,1024,256]{2,1,0:T(8,128)}, bf16[4,1024,256]{2,1,0:T(8,128)(2,1)}, bf16[4,1024,256]{2,1,0:T(8,128)(2,1)}, f32[1,4]{1,0:T(1,128)}, f32[2,4]{1,0:T(2,128)}, /*index=5*/f32[2,4]{1,0:T(2,128)}) custom-call(f32[4,1024,256]{2,1,0:T(8,128)S(1)} %get-tuple-element.20.par, bf16[4,1024,256]{2,1,0:T(8,128)(2,1)S(1)} %get-tuple-element.21.qm, ...), custom_call_target="tpu_custom_call" | custom-call | tf_op jit(solution)/shard_map/pallas_call | solution.py:604

commit v5 on v4

--- a/solution.py
+++ b/solution.py
@@ -14,7 +14,7 @@
 SPLIT = 1
 SLOTS = 3
 RING = 4
-Z_RING = 16
+Z_RING = 12
 LEAD = 0
 CHAIN_AT = 3
 LAG_A = 4
@@ -354,7 +354,7 @@
         update(t, c, lambda at: gathered(t, c, at) + (y_in[s, z, c, at, :] + mine(t, z, y, c, at)))
 
     def row_copy(t, o):
-        h = lax.rem(t, 2)
+        h = t % 2 if isinstance(t, int) else lax.rem(t, 2)
         return pltpu.make_async_remote_copy(
             src_ref=row.at[h], dst_ref=row_in.at[h, o], send_sem=st_send.at[h], recv_sem=st_recv.at[h],
             device_id={"tensor": lax.rem(mt + o // n, peers), "dp": lax.rem(me + lax.rem(o, n), n)},
@@ -376,7 +376,11 @@
         best = jnp.broadcast_to(jnp.max(stat[t], axis=1, keepdims=True), (kinds, lanes))
         at = [lax.broadcasted_iota(jnp.int32, (kinds, lanes), i) for i in range(2)]
         row[h] = jnp.max(jnp.where(at[0] == at[1], best, -jnp.inf), axis=0, keepdims=True)
-        each(1, n * peers, lambda o: row_copy(t, n * peers - o).start())
+        if isinstance(t, int):
+            for o in reversed(range(1, n * peers)):
+                row_copy(t, o).start()
+        else:
+            each(1, n * peers, lambda o: row_copy(t, n * peers - o).start())
 
     def all_rows(body):
         def one(i, _):
@@ -400,6 +404,7 @@
     lag_a = jnp.where(is_inner, LAG_A, -LEAD)
     lag_b = jnp.where(is_inner, LAG_B_INNER, LAG_B)
     own = wide * (nz - 1) + sides
+    idle = own + wide - n_b(z)
 
     def place(g, lag):
         g = g - lag
@@ -434,8 +439,8 @@
         ok, t, p = place(g, 0)
         tail = p >= own
         i = jnp.where(tail, nz - 1, p // wide)
-        c = jnp.where(tail, p - own, lax.rem(p, wide))
-        live = ok & (tail | (p < own - sides)) & (c < n_b(order(i)))
+        c = jnp.where(tail, p - idle, lax.rem(p, wide))
+        live = ok & (tail | (p < own - sides)) & (c >= 0) & (c < n_b(order(i)))
 
         @pl.when(live)
         def _():
@@ -477,9 +482,9 @@
         @pl.when(ok & (c >= 0) & (c < n_a(z)) & (p < own))
         def _():
             update_a(t, c)
-        c = p - own
-
-        @pl.when(ok & (c >= 0) & (c < n_b(z)))
+        c = p - idle
+
+        @pl.when(ok & (c >= 0) & (p >= own))
         def _():
             update_b(t, c)
 

time: 333 us -> 333 us (level)
  no operation moved by 1% of the time
where the time goes in v5:
time: 333 us
  Pallas kernels  332 us (100%)
    pallas_call x1, Pallas kernels, on_device(): pl.pallas_call(functools.partial(kernel, n, peers), out_shape=(pltpu.VMEM...  329 us

profile of v5, /device:TPU:0, one launch (start us, length us, event | category | flops | bytes accessed | tf_op | source)
XLA Modules:
  0.0 332.9 jit_solution(10452249395349798258)
XLA Ops:
  0.6 328.9 %shard_map.118 = (f32[4,1024,256]{2,1,0:T(8,128)S(1)}, bf16[4,1024,256]{2,1,0:T(8,128)(2,1)S(1)}, bf16[4,1024,256]{2,1,0:T(8,128)(2,1)S(1)}, f32[2,1024,256]{2,1...) custom-call(bf16[4,8,1024,256]{3,2,1,0:T(8,128)(2,1)} %bitcast.6, ...), custom_call_target="tpu_custom_call" | custom-call | tf_op jit(solution)/shard_map/pallas_call | solution.py:584
  329.5 3.4 %shard_map.119 = (f32[4,1024,256]{2,1,0:T(8,128)}, bf16[4,1024,256]{2,1,0:T(8,128)(2,1)}, bf16[4,1024,256]{2,1,0:T(8,128)(2,1)}, f32[1,4]{1,0:T(1,128)}, f32[2,4]{1,0:T(2,128)}, /*index=5*/f32[2,4]{1,0:T(2,128)}) custom-call(f32[4,1024,256]{2,1,0:T(8,128)S(1)} %get-tuple-element.20.par, bf16[4,1024,256]{2,1,0:T(8,128)(2,1)S(1)} %get-tuple-element.21.qm, ...), custom_call_target="tpu_custom_call" | custom-call | tf_op jit(solution)/shard_map/pallas_call | solution.py:609
